TPU v7x, 32 devices: a 4x4x1 block of a 4x4x8 slice. The times are simulated.
32 devices in a mesh: batch: 1 (over z), cols: 4 (over y), rows: 8 (over x, core).
Axes of the slice: x: 4, y: 4, z: 1, core: 2. Of those that a mesh axis runs over, the one named last changes fastest.
The devices are a block of a 4x4x8 slice.
Arguments:
- frames: bfloat16 [12, 2, 192, 96, 16], P(None, 'batch', 'rows', 'cols')
- w_x: bfloat16 [3, 3, 16, 512], replicated
- w_h: bfloat16 [3, 3, 128, 512], replicated
- gate_bias: float32 [512], replicated
- h_init: bfloat16 [2, 192, 96, 128], P('batch', 'rows', 'cols')
- c_init: float32 [2, 192, 96, 128], P('batch', 'rows', 'cols')
Outputs:
- output 1: bfloat16 [12, 2, 192, 96, 128], P(None, 'batch', 'rows', 'cols')
- output 2: float32 [2, 192, 96, 128], P('batch', 'rows', 'cols')
All inputs are finite; a program needn't handle non-finite values.
Results may differ from a plain program's by a relative error of at most 0.00230549.
Values are sent between devices in bfloat16 or wider.
A program may use at most 768 MiB of HBM per device.

v0:
```python
import jax
import jax.numpy as jnp
from jax import lax
from jax.sharding import PartitionSpec as P, NamedSharding


def edge_swap(tile_arr, halo_width, split_dim, axis_label, axis_count):
    length = tile_arr.shape[split_dim]
    low_edge = lax.slice_in_dim(tile_arr, 0, halo_width, axis=split_dim)
    high_edge = lax.slice_in_dim(tile_arr, length - halo_width, length, axis=split_dim)
    down_pairs = [(source, source + 1) for source in range(axis_count - 1)]
    up_pairs = [(source + 1, source) for source in range(axis_count - 1)]
    from_prev = lax.ppermute(high_edge, axis_label, down_pairs)
    from_next = lax.ppermute(low_edge, axis_label, up_pairs)
    return jnp.concatenate([from_prev, tile_arr, from_next], axis=split_dim)


def with_halo(tile_arr, halo_width, row_dim, row_count, col_count):
    row_ext = edge_swap(tile_arr, halo_width, row_dim, "rows", row_count)
    return edge_swap(row_ext, halo_width, row_dim + 1, "cols", col_count)


def conv_taps(padded, weights, out_rows, out_cols):
    tap_list = [padded[:, row_off:row_off + out_rows, col_off:col_off + out_cols, :] for row_off in range(3) for col_off in range(3)]
    patches = jnp.concatenate(tap_list, axis=-1)
    flat_patches = patches.reshape(-1, patches.shape[-1])
    flat_weights = weights.reshape(-1, weights.shape[-1])
    product = jnp.dot(flat_patches, flat_weights, preferred_element_type=jnp.float32)
    return product.reshape(padded.shape[0], out_rows, out_cols, -1)


def lstm_cell(gate_sum, cell_prev):
    hidden_width = cell_prev.shape[-1]
    in_gate = jax.nn.sigmoid(gate_sum[..., :hidden_width])
    forget_gate = jax.nn.sigmoid(gate_sum[..., hidden_width:2 * hidden_width])
    out_gate = jax.nn.sigmoid(gate_sum[..., 2 * hidden_width:3 * hidden_width])
    cand_gate = jnp.tanh(gate_sum[..., 3 * hidden_width:])
    cell_next = forget_gate * cell_prev + in_gate * cand_gate
    hidden_next = (out_gate * jnp.tanh(cell_next)).astype(jnp.bfloat16)
    return hidden_next, cell_next


def solution(mesh):
    row_count = mesh.shape["rows"]
    col_count = mesh.shape["cols"]
    frame_spec = P(None, "batch", "rows", "cols", None)
    state_spec = P("batch", "rows", "cols", None)

    def local_run(frames, w_x, w_h, gate_bias, h_init, c_init):
        tile_rows = h_init.shape[1]
        tile_cols = h_init.shape[2]
        frames_ext = with_halo(frames, 1, 2, row_count, col_count)

        def step_fn(state_pair, frame_ext):
            hidden, cell_state = state_pair
            hidden_ext = with_halo(hidden, 1, 1, row_count, col_count)
            gate_sum = conv_taps(frame_ext, w_x, tile_rows, tile_cols) + conv_taps(hidden_ext, w_h, tile_rows, tile_cols) + gate_bias
            hidden_next, cell_next = lstm_cell(gate_sum, cell_state)
            return (hidden_next, cell_next), hidden_next

        final_pair, all_hidden = lax.scan(step_fn, (h_init, c_init), frames_ext)
        return all_hidden, final_pair[1]

    return jax.shard_map(local_run, mesh=mesh, in_specs=(frame_spec, P(), P(), P(), state_spec, state_spec), out_specs=(frame_spec, state_spec), check_vma=False)
```

profile of v0, /device:TPU:97, one launch (start us, length us, event | category | flops | bytes accessed | tf_op | source)
XLA Modules:
  0.0 325.8 jit_solution(9174228454930845900)
XLA Ops:
  2.5 3.4 %copy.8 = bf16[12,2,24,24,16]{4,3,2,1,0:T(8,128)(2,1)S(1)} copy(bf16[12,2,24,24,16]{3,4,2,1,0:T(8,128)(2,1)} %param.8) | data formatting | bytes 884736 | tf_op args[0]
  6.0 4.6 %collective-permute-start.4 = (bf16[12,2,1,24,16]{4,3,2,1,0:T(8,128)(2,1)S(1)}, bf16[12,2,1,24,16]{4,3,2,1,0:T(8,128)(2,1)S(1)}, u32[]{:S(2)}, u32[]{:S(2)}) collective-permute-start(bf16[12,2,1,24,16]{4,3,2,1,0:T(8,128)(2,1)S(1)} %get-tuple-element.81), channel_id=1, source_target_pairs={{0,1},{1,2},{2,3},{3,4},{4,5},{5,6},{6,7},{8,9},{9,10},{10,11},{11... | collective-permute-start | bytes 55304 | tf_op jit(solution)/shard_map/ppermute | solution.py:13
  12.7 4.4 %collective-permute-done.5 = bf16[12,2,1,24,16]{4,3,2,1,0:T(8,128)(2,1)S(1)} collective-permute-done((bf16[12,2,1,24,16]{4,3,2,1,0:T(8,128)(2,1)S(1)}, bf16[12,2,1,24,16]{4,3,2,1,0:T(8,128)(2,1)S(1)}, u32[]{:S(2)}, u32[]{:S(2)}) %collective-permute-start.5) | collective-permute-done | bytes 18464 | tf_op jit(solution)/shard_map/ppermute | solution.py:14
  18.7 4.5 %collective-permute-start.6 = (bf16[12,2,26,1,16]{4,3,2,1,0:T(2,128)(2,1)}, bf16[12,2,26,1,16]{4,3,2,1,0:T(2,128)(2,1)}, u32[]{:S(2)}, u32[]{:S(2)}) collective-permute-start(bf16[12,2,26,1,16]{4,3,2,1,0:T(2,128)(2,1)} %get-tuple-element.79), channel_id=1, source_target_pairs={{0,8},{8,16},{16,24},{1,9},{9,17},{17,25},{2,10},{10,18},{18,26},{... | collective-permute-start | bytes 59912 | tf_op jit(solution)/shard_map/ppermute | solution.py:13
  24.5 2.5 collective-permute-done.6
  27.0 4.9 %collective-permute-done.7 = bf16[12,2,26,1,16]{4,3,2,1,0:T(2,128)(2,1)} collective-permute-done((bf16[12,2,26,1,16]{4,3,2,1,0:T(2,128)(2,1)}, bf16[12,2,26,1,16]{4,3,2,1,0:T(2,128)(2,1)}, u32[]{:S(2)}, u32[]{:S(2)}) %collective-permute-start.7) | collective-permute-done | bytes 20000 | tf_op jit(solution)/shard_map/ppermute | solution.py:14
  31.9 6.6 %pad_maximum_fusion.4 = bf16[12,2,26,26,16]{4,3,2,1,0:T(8,128)(2,1)} fusion(bf16[12,2,26,1,16]{4,3,2,1,0:T(2,128)(2,1)} %collective-permute-done.7, bf16[12,2,1,24,16]{4,3,2,1,0:T(8,128)(2,1)} %copy-done.6, bf16[12,2,24,24,16]{4,3,2,1,0:T(8,128)(2,1)} %copy-done.1, bf16[12,2,1,24,16]{4,3,2,1,0:T(8,128)(2,1)} %copy-done.5, ...), kind=kLoop, calls=%fused_computation.49 | loop fusion | flops 2595840 | bytes 1038336 | tf_op jit(solution)/shard_map/concatenate | solution.py:15
  38.6 287.2 %while.14 = (s32[]{:T(128)}, bf16[2,24,24,128]{3,2,1,0:T(8,128)(2,1)S(1)}, f32[2,24,24,128]{3,2,1,0:T(8,128)}, bf16[12,2,24,24,128]{4,3,2,1,0:T(8,128)(2,1)}, bf...) while((s32[]{:T(128)}, ...), condition=%wide.region_1.2_spmd, body=%wide.region_0.1_spmd.sunk | while | flops 1536786432 | bytes 32946016 | solution.py:61
  38.6 5.0 %collective-permute-start = (bf16[2,1,24,128]{3,2,1,0:T(8,128)(2,1)S(1)}, bf16[2,1,24,128]{3,2,1,0:T(8,128)(2,1)S(1)}, u32[]{:S(2)}, u32[]{:S(2)}) collective-permute-start(bf16[2,1,24,128]{3,2,1,0:T(8,128)(2,1)S(1)} %get-tuple-element.157), channel_id=1, source_target_pairs={{0,1},{1,2},{2,3},{3,4},{4,5},{5,6},{6,7},{8,9},{9,10},{10,11},{11... | collective-permute-start | bytes 36872 | tf_op jit(solution)/shard_map/while/body/eval_jaxpr/ppermute | solution.py:13
  43.6 2.0 collective-permute-start.1
  47.0 2.2 concatenate.35
  49.4 3.0 collective-permute-start.2
  55.4 3.3 collective-permute-done.3
  63.7 4.9 %collective-permute-start = (bf16[2,1,24,128]{3,2,1,0:T(8,128)(2,1)S(1)}, bf16[2,1,24,128]{3,2,1,0:T(8,128)(2,1)S(1)}, u32[]{:S(2)}, u32[]{:S(2)}) collective-permute-start(bf16[2,1,24,128]{3,2,1,0:T(8,128)(2,1)S(1)} %get-tuple-element.157), channel_id=1, source_target_pairs={{0,1},{1,2},{2,3},{3,4},{4,5},{5,6},{6,7},{8,9},{9,10},{10,11},{11... | collective-permute-start | bytes 36872 | tf_op jit(solution)/shard_map/while/body/eval_jaxpr/ppermute | solution.py:13
  71.9 2.2 concatenate.35
  74.3 3.6 %collective-permute-start.2 = (bf16[2,26,1,128]{3,2,1,0:T(2,128)(2,1)S(1)}, bf16[2,26,1,128]{3,2,1,0:T(2,128)(2,1)S(1)}, u32[]{:S(2)}, u32[]{:S(2)}) collective-permute-start(bf16[2,26,1,128]{3,2,1,0:T(2,128)(2,1)S(1)} %get-tuple-element.159), channel_id=1, source_target_pairs={{0,8},{8,16},{16,24},{1,9},{9,17},{17,25},{2,10},{10,18},{18,26},{... | collective-permute-start | bytes 39944 | tf_op jit(solution)/shard_map/while/body/eval_jaxpr/ppermute | solution.py:13
  81.0 3.1 collective-permute-done.3
  89.1 5.1 %collective-permute-start = (bf16[2,1,24,128]{3,2,1,0:T(8,128)(2,1)S(1)}, bf16[2,1,24,128]{3,2,1,0:T(8,128)(2,1)S(1)}, u32[]{:S(2)}, u32[]{:S(2)}) collective-permute-start(bf16[2,1,24,128]{3,2,1,0:T(8,128)(2,1)S(1)} %get-tuple-element.157), channel_id=1, source_target_pairs={{0,1},{1,2},{2,3},{3,4},{4,5},{5,6},{6,7},{8,9},{9,10},{10,11},{11... | collective-permute-start | bytes 36872 | tf_op jit(solution)/shard_map/while/body/eval_jaxpr/ppermute | solution.py:13
  94.2 2.0 collective-permute-start.1
  97.5 2.2 concatenate.35
  104.7 3.1 collective-permute-done.3
  112.7 5.1 %collective-permute-start = (bf16[2,1,24,128]{3,2,1,0:T(8,128)(2,1)S(1)}, bf16[2,1,24,128]{3,2,1,0:T(8,128)(2,1)S(1)}, u32[]{:S(2)}, u32[]{:S(2)}) collective-permute-start(bf16[2,1,24,128]{3,2,1,0:T(8,128)(2,1)S(1)} %get-tuple-element.157), channel_id=1, source_target_pairs={{0,1},{1,2},{2,3},{3,4},{4,5},{5,6},{6,7},{8,9},{9,10},{10,11},{11... | collective-permute-start | bytes 36872 | tf_op jit(solution)/shard_map/while/body/eval_jaxpr/ppermute | solution.py:13
  121.2 2.2 concatenate.35
  128.3 3.1 collective-permute-done.3
  136.4 5.1 %collective-permute-start = (bf16[2,1,24,128]{3,2,1,0:T(8,128)(2,1)S(1)}, bf16[2,1,24,128]{3,2,1,0:T(8,128)(2,1)S(1)}, u32[]{:S(2)}, u32[]{:S(2)}) collective-permute-start(bf16[2,1,24,128]{3,2,1,0:T(8,128)(2,1)S(1)} %get-tuple-element.157), channel_id=1, source_target_pairs={{0,1},{1,2},{2,3},{3,4},{4,5},{5,6},{6,7},{8,9},{9,10},{10,11},{11... | collective-permute-start | bytes 36872 | tf_op jit(solution)/shard_map/while/body/eval_jaxpr/ppermute | solution.py:13
  144.9 2.2 concatenate.35
  152.0 3.1 collective-permute-done.3
  160.1 5.1 %collective-permute-start = (bf16[2,1,24,128]{3,2,1,0:T(8,128)(2,1)S(1)}, bf16[2,1,24,128]{3,2,1,0:T(8,128)(2,1)S(1)}, u32[]{:S(2)}, u32[]{:S(2)}) collective-permute-start(bf16[2,1,24,128]{3,2,1,0:T(8,128)(2,1)S(1)} %get-tuple-element.157), channel_id=1, source_target_pairs={{0,1},{1,2},{2,3},{3,4},{4,5},{5,6},{6,7},{8,9},{9,10},{10,11},{11... | collective-permute-start | bytes 36872 | tf_op jit(solution)/shard_map/while/body/eval_jaxpr/ppermute | solution.py:13
  168.5 2.2 concatenate.35
  175.7 3.1 collective-permute-done.3
  183.7 5.1 %collective-permute-start = (bf16[2,1,24,128]{3,2,1,0:T(8,128)(2,1)S(1)}, bf16[2,1,24,128]{3,2,1,0:T(8,128)(2,1)S(1)}, u32[]{:S(2)}, u32[]{:S(2)}) collective-permute-start(bf16[2,1,24,128]{3,2,1,0:T(8,128)(2,1)S(1)} %get-tuple-element.157), channel_id=1, source_target_pairs={{0,1},{1,2},{2,3},{3,4},{4,5},{5,6},{6,7},{8,9},{9,10},{10,11},{11... | collective-permute-start | bytes 36872 | tf_op jit(solution)/shard_map/while/body/eval_jaxpr/ppermute | solution.py:13
  192.2 2.2 concatenate.35
  199.4 3.1 collective-permute-done.3
  207.4 5.1 %collective-permute-start = (bf16[2,1,24,128]{3,2,1,0:T(8,128)(2,1)S(1)}, bf16[2,1,24,128]{3,2,1,0:T(8,128)(2,1)S(1)}, u32[]{:S(2)}, u32[]{:S(2)}) collective-permute-start(bf16[2,1,24,128]{3,2,1,0:T(8,128)(2,1)S(1)} %get-tuple-element.157), channel_id=1, source_target_pairs={{0,1},{1,2},{2,3},{3,4},{4,5},{5,6},{6,7},{8,9},{9,10},{10,11},{11... | collective-permute-start | bytes 36872 | tf_op jit(solution)/shard_map/while/body/eval_jaxpr/ppermute | solution.py:13
  215.9 2.2 concatenate.35
  223.0 3.1 collective-permute-done.3
  231.1 5.1 %collective-permute-start = (bf16[2,1,24,128]{3,2,1,0:T(8,128)(2,1)S(1)}, bf16[2,1,24,128]{3,2,1,0:T(8,128)(2,1)S(1)}, u32[]{:S(2)}, u32[]{:S(2)}) collective-permute-start(bf16[2,1,24,128]{3,2,1,0:T(8,128)(2,1)S(1)} %get-tuple-element.157), channel_id=1, source_target_pairs={{0,1},{1,2},{2,3},{3,4},{4,5},{5,6},{6,7},{8,9},{9,10},{10,11},{11... | collective-permute-start | bytes 36872 | tf_op jit(solution)/shard_map/while/body/eval_jaxpr/ppermute | solution.py:13
  239.5 2.2 concatenate.35
  246.7 3.1 collective-permute-done.3
  254.8 5.1 %collective-permute-start = (bf16[2,1,24,128]{3,2,1,0:T(8,128)(2,1)S(1)}, bf16[2,1,24,128]{3,2,1,0:T(8,128)(2,1)S(1)}, u32[]{:S(2)}, u32[]{:S(2)}) collective-permute-start(bf16[2,1,24,128]{3,2,1,0:T(8,128)(2,1)S(1)} %get-tuple-element.157), channel_id=1, source_target_pairs={{0,1},{1,2},{2,3},{3,4},{4,5},{5,6},{6,7},{8,9},{9,10},{10,11},{11... | collective-permute-start | bytes 36872 | tf_op jit(solution)/shard_map/while/body/eval_jaxpr/ppermute | solution.py:13
  263.2 2.2 concatenate.35
  270.4 3.1 collective-permute-done.3
  278.4 5.1 %collective-permute-start = (bf16[2,1,24,128]{3,2,1,0:T(8,128)(2,1)S(1)}, bf16[2,1,24,128]{3,2,1,0:T(8,128)(2,1)S(1)}, u32[]{:S(2)}, u32[]{:S(2)}) collective-permute-start(bf16[2,1,24,128]{3,2,1,0:T(8,128)(2,1)S(1)} %get-tuple-element.157), channel_id=1, source_target_pairs={{0,1},{1,2},{2,3},{3,4},{4,5},{5,6},{6,7},{8,9},{9,10},{10,11},{11... | collective-permute-start | bytes 36872 | tf_op jit(solution)/shard_map/while/body/eval_jaxpr/ppermute | solution.py:13
  286.9 2.2 concatenate.35
  294.0 3.1 collective-permute-done.3
  302.1 5.1 %collective-permute-start = (bf16[2,1,24,128]{3,2,1,0:T(8,128)(2,1)S(1)}, bf16[2,1,24,128]{3,2,1,0:T(8,128)(2,1)S(1)}, u32[]{:S(2)}, u32[]{:S(2)}) collective-permute-start(bf16[2,1,24,128]{3,2,1,0:T(8,128)(2,1)S(1)} %get-tuple-element.157), channel_id=1, source_target_pairs={{0,1},{1,2},{2,3},{3,4},{4,5},{5,6},{6,7},{8,9},{9,10},{10,11},{11... | collective-permute-start | bytes 36872 | tf_op jit(solution)/shard_map/while/body/eval_jaxpr/ppermute | solution.py:13
  310.6 2.2 concatenate.35
  317.7 3.1 collective-permute-done.3
  (387 shorter events, 157.0 us)
Async XLA Ops:
  6.0 6.7 %collective-permute-start.4 = (bf16[12,2,1,24,16]{4,3,2,1,0:T(8,128)(2,1)S(1)}, bf16[12,2,1,24,16]{4,3,2,1,0:T(8,128)(2,1)S(1)}, u32[]{:S(2)}, u32[]{:S(2)}) collective-permute-start(bf16[12,2,1,24,16]{4,3,2,1,0:T(8,128)(2,1)S(1)} %get-tuple-element.81), channel_id=1, source_target_pairs={{0,1},{1,2},{2,3},{3,4},{4,5},{5,6},{6,7},{8,9},{9,10},{10,11},{11... | collective-permute-start | bytes 55304 | tf_op jit(solution)/shard_map/ppermute | solution.py:13
  10.6 6.5 %collective-permute-start.5 = (bf16[12,2,1,24,16]{4,3,2,1,0:T(8,128)(2,1)S(1)}, bf16[12,2,1,24,16]{4,3,2,1,0:T(8,128)(2,1)S(1)}, u32[]{:S(2)}, u32[]{:S(2)}) collective-permute-start(bf16[12,2,1,24,16]{4,3,2,1,0:T(8,128)(2,1)S(1)} %get-tuple-element.82), channel_id=1, source_target_pairs={{1,0},{2,1},{3,2},{4,3},{5,4},{6,5},{7,6},{9,8},{10,9},{11,10},{12... | collective-permute-start | bytes 55304 | tf_op jit(solution)/shard_map/ppermute | solution.py:14
  18.7 8.4 %collective-permute-start.6 = (bf16[12,2,26,1,16]{4,3,2,1,0:T(2,128)(2,1)}, bf16[12,2,26,1,16]{4,3,2,1,0:T(2,128)(2,1)}, u32[]{:S(2)}, u32[]{:S(2)}) collective-permute-start(bf16[12,2,26,1,16]{4,3,2,1,0:T(2,128)(2,1)} %get-tuple-element.79), channel_id=1, source_target_pairs={{0,8},{8,16},{16,24},{1,9},{9,17},{17,25},{2,10},{10,18},{18,26},{... | collective-permute-start | bytes 59912 | tf_op jit(solution)/shard_map/ppermute | solution.py:13
  23.2 8.7 %collective-permute-start.7 = (bf16[12,2,26,1,16]{4,3,2,1,0:T(2,128)(2,1)}, bf16[12,2,26,1,16]{4,3,2,1,0:T(2,128)(2,1)}, u32[]{:S(2)}, u32[]{:S(2)}) collective-permute-start(bf16[12,2,26,1,16]{4,3,2,1,0:T(2,128)(2,1)} %get-tuple-element.80), channel_id=1, source_target_pairs={{8,0},{16,8},{24,16},{9,1},{17,9},{25,17},{10,2},{18,10},{26,18},{... | collective-permute-start | bytes 59912 | tf_op jit(solution)/shard_map/ppermute | solution.py:14
  38.6 10.6 %collective-permute-start = (bf16[2,1,24,128]{3,2,1,0:T(8,128)(2,1)S(1)}, bf16[2,1,24,128]{3,2,1,0:T(8,128)(2,1)S(1)}, u32[]{:S(2)}, u32[]{:S(2)}) collective-permute-start(bf16[2,1,24,128]{3,2,1,0:T(8,128)(2,1)S(1)} %get-tuple-element.157), channel_id=1, source_target_pairs={{0,1},{1,2},{2,3},{3,4},{4,5},{5,6},{6,7},{8,9},{9,10},{10,11},{11... | collective-permute-start | bytes 36872 | tf_op jit(solution)/shard_map/while/body/eval_jaxpr/ppermute | solution.py:13
  43.6 5.7 %collective-permute-start.1 = (bf16[2,1,24,128]{3,2,1,0:T(8,128)(2,1)S(1)}, bf16[2,1,24,128]{3,2,1,0:T(8,128)(2,1)S(1)}, u32[]{:S(2)}, u32[]{:S(2)}) collective-permute-start(bf16[2,1,24,128]{3,2,1,0:T(8,128)(2,1)S(1)} %get-tuple-element.158), channel_id=1, source_target_pairs={{1,0},{2,1},{3,2},{4,3},{5,4},{6,5},{7,6},{9,8},{10,9},{11,10},{12... | collective-permute-start | bytes 36872 | tf_op jit(solution)/shard_map/while/body/eval_jaxpr/ppermute | solution.py:14
  49.4 5.8 %collective-permute-start.2 = (bf16[2,26,1,128]{3,2,1,0:T(2,128)(2,1)S(1)}, bf16[2,26,1,128]{3,2,1,0:T(2,128)(2,1)S(1)}, u32[]{:S(2)}, u32[]{:S(2)}) collective-permute-start(bf16[2,26,1,128]{3,2,1,0:T(2,128)(2,1)S(1)} %get-tuple-element.159), channel_id=1, source_target_pairs={{0,8},{8,16},{16,24},{1,9},{9,17},{17,25},{2,10},{10,18},{18,26},{... | collective-permute-start | bytes 39944 | tf_op jit(solution)/shard_map/while/body/eval_jaxpr/ppermute | solution.py:13
  53.9 4.8 %collective-permute-start.3 = (bf16[2,26,1,128]{3,2,1,0:T(2,128)(2,1)S(1)}, bf16[2,26,1,128]{3,2,1,0:T(2,128)(2,1)S(1)}, u32[]{:S(2)}, u32[]{:S(2)}) collective-permute-start(bf16[2,26,1,128]{3,2,1,0:T(2,128)(2,1)S(1)} %get-tuple-element.160), channel_id=1, source_target_pairs={{8,0},{16,8},{24,16},{9,1},{17,9},{25,17},{10,2},{18,10},{26,18},{... | collective-permute-start | bytes 39944 | tf_op jit(solution)/shard_map/while/body/eval_jaxpr/ppermute | solution.py:14
  63.7 10.5 %collective-permute-start = (bf16[2,1,24,128]{3,2,1,0:T(8,128)(2,1)S(1)}, bf16[2,1,24,128]{3,2,1,0:T(8,128)(2,1)S(1)}, u32[]{:S(2)}, u32[]{:S(2)}) collective-permute-start(bf16[2,1,24,128]{3,2,1,0:T(8,128)(2,1)S(1)} %get-tuple-element.157), channel_id=1, source_target_pairs={{0,1},{1,2},{2,3},{3,4},{4,5},{5,6},{6,7},{8,9},{9,10},{10,11},{11... | collective-permute-start | bytes 36872 | tf_op jit(solution)/shard_map/while/body/eval_jaxpr/ppermute | solution.py:13
  68.6 5.7 %collective-permute-start.1 = (bf16[2,1,24,128]{3,2,1,0:T(8,128)(2,1)S(1)}, bf16[2,1,24,128]{3,2,1,0:T(8,128)(2,1)S(1)}, u32[]{:S(2)}, u32[]{:S(2)}) collective-permute-start(bf16[2,1,24,128]{3,2,1,0:T(8,128)(2,1)S(1)} %get-tuple-element.158), channel_id=1, source_target_pairs={{1,0},{2,1},{3,2},{4,3},{5,4},{6,5},{7,6},{9,8},{10,9},{11,10},{12... | collective-permute-start | bytes 36872 | tf_op jit(solution)/shard_map/while/body/eval_jaxpr/ppermute | solution.py:14
  74.3 6.4 %collective-permute-start.2 = (bf16[2,26,1,128]{3,2,1,0:T(2,128)(2,1)S(1)}, bf16[2,26,1,128]{3,2,1,0:T(2,128)(2,1)S(1)}, u32[]{:S(2)}, u32[]{:S(2)}) collective-permute-start(bf16[2,26,1,128]{3,2,1,0:T(2,128)(2,1)S(1)} %get-tuple-element.159), channel_id=1, source_target_pairs={{0,8},{8,16},{16,24},{1,9},{9,17},{17,25},{2,10},{10,18},{18,26},{... | collective-permute-start | bytes 39944 | tf_op jit(solution)/shard_map/while/body/eval_jaxpr/ppermute | solution.py:13
  79.4 4.6 %collective-permute-start.3 = (bf16[2,26,1,128]{3,2,1,0:T(2,128)(2,1)S(1)}, bf16[2,26,1,128]{3,2,1,0:T(2,128)(2,1)S(1)}, u32[]{:S(2)}, u32[]{:S(2)}) collective-permute-start(bf16[2,26,1,128]{3,2,1,0:T(2,128)(2,1)S(1)} %get-tuple-element.160), channel_id=1, source_target_pairs={{8,0},{16,8},{24,16},{9,1},{17,9},{25,17},{10,2},{18,10},{26,18},{... | collective-permute-start | bytes 39944 | tf_op jit(solution)/shard_map/while/body/eval_jaxpr/ppermute | solution.py:14
  89.1 10.7 %collective-permute-start = (bf16[2,1,24,128]{3,2,1,0:T(8,128)(2,1)S(1)}, bf16[2,1,24,128]{3,2,1,0:T(8,128)(2,1)S(1)}, u32[]{:S(2)}, u32[]{:S(2)}) collective-permute-start(bf16[2,1,24,128]{3,2,1,0:T(8,128)(2,1)S(1)} %get-tuple-element.157), channel_id=1, source_target_pairs={{0,1},{1,2},{2,3},{3,4},{4,5},{5,6},{6,7},{8,9},{9,10},{10,11},{11... | collective-permute-start | bytes 36872 | tf_op jit(solution)/shard_map/while/body/eval_jaxpr/ppermute | solution.py:13
  94.2 5.7 %collective-permute-start.1 = (bf16[2,1,24,128]{3,2,1,0:T(8,128)(2,1)S(1)}, bf16[2,1,24,128]{3,2,1,0:T(8,128)(2,1)S(1)}, u32[]{:S(2)}, u32[]{:S(2)}) collective-permute-start(bf16[2,1,24,128]{3,2,1,0:T(8,128)(2,1)S(1)} %get-tuple-element.158), channel_id=1, source_target_pairs={{1,0},{2,1},{3,2},{4,3},{5,4},{6,5},{7,6},{9,8},{10,9},{11,10},{12... | collective-permute-start | bytes 36872 | tf_op jit(solution)/shard_map/while/body/eval_jaxpr/ppermute | solution.py:14
  99.9 4.5 %collective-permute-start.2 = (bf16[2,26,1,128]{3,2,1,0:T(2,128)(2,1)S(1)}, bf16[2,26,1,128]{3,2,1,0:T(2,128)(2,1)S(1)}, u32[]{:S(2)}, u32[]{:S(2)}) collective-permute-start(bf16[2,26,1,128]{3,2,1,0:T(2,128)(2,1)S(1)} %get-tuple-element.159), channel_id=1, source_target_pairs={{0,8},{8,16},{16,24},{1,9},{9,17},{17,25},{2,10},{10,18},{18,26},{... | collective-permute-start | bytes 39944 | tf_op jit(solution)/shard_map/while/body/eval_jaxpr/ppermute | solution.py:13
  103.1 4.6 %collective-permute-start.3 = (bf16[2,26,1,128]{3,2,1,0:T(2,128)(2,1)S(1)}, bf16[2,26,1,128]{3,2,1,0:T(2,128)(2,1)S(1)}, u32[]{:S(2)}, u32[]{:S(2)}) collective-permute-start(bf16[2,26,1,128]{3,2,1,0:T(2,128)(2,1)S(1)} %get-tuple-element.160), channel_id=1, source_target_pairs={{8,0},{16,8},{24,16},{9,1},{17,9},{25,17},{10,2},{18,10},{26,18},{... | collective-permute-start | bytes 39944 | tf_op jit(solution)/shard_map/while/body/eval_jaxpr/ppermute | solution.py:14
  112.7 10.7 %collective-permute-start = (bf16[2,1,24,128]{3,2,1,0:T(8,128)(2,1)S(1)}, bf16[2,1,24,128]{3,2,1,0:T(8,128)(2,1)S(1)}, u32[]{:S(2)}, u32[]{:S(2)}) collective-permute-start(bf16[2,1,24,128]{3,2,1,0:T(8,128)(2,1)S(1)} %get-tuple-element.157), channel_id=1, source_target_pairs={{0,1},{1,2},{2,3},{3,4},{4,5},{5,6},{6,7},{8,9},{9,10},{10,11},{11... | collective-permute-start | bytes 36872 | tf_op jit(solution)/shard_map/while/body/eval_jaxpr/ppermute | solution.py:13
  117.8 5.7 %collective-permute-start.1 = (bf16[2,1,24,128]{3,2,1,0:T(8,128)(2,1)S(1)}, bf16[2,1,24,128]{3,2,1,0:T(8,128)(2,1)S(1)}, u32[]{:S(2)}, u32[]{:S(2)}) collective-permute-start(bf16[2,1,24,128]{3,2,1,0:T(8,128)(2,1)S(1)} %get-tuple-element.158), channel_id=1, source_target_pairs={{1,0},{2,1},{3,2},{4,3},{5,4},{6,5},{7,6},{9,8},{10,9},{11,10},{12... | collective-permute-start | bytes 36872 | tf_op jit(solution)/shard_map/while/body/eval_jaxpr/ppermute | solution.py:14
  123.6 4.5 %collective-permute-start.2 = (bf16[2,26,1,128]{3,2,1,0:T(2,128)(2,1)S(1)}, bf16[2,26,1,128]{3,2,1,0:T(2,128)(2,1)S(1)}, u32[]{:S(2)}, u32[]{:S(2)}) collective-permute-start(bf16[2,26,1,128]{3,2,1,0:T(2,128)(2,1)S(1)} %get-tuple-element.159), channel_id=1, source_target_pairs={{0,8},{8,16},{16,24},{1,9},{9,17},{17,25},{2,10},{10,18},{18,26},{... | collective-permute-start | bytes 39944 | tf_op jit(solution)/shard_map/while/body/eval_jaxpr/ppermute | solution.py:13
  126.8 4.6 %collective-permute-start.3 = (bf16[2,26,1,128]{3,2,1,0:T(2,128)(2,1)S(1)}, bf16[2,26,1,128]{3,2,1,0:T(2,128)(2,1)S(1)}, u32[]{:S(2)}, u32[]{:S(2)}) collective-permute-start(bf16[2,26,1,128]{3,2,1,0:T(2,128)(2,1)S(1)} %get-tuple-element.160), channel_id=1, source_target_pairs={{8,0},{16,8},{24,16},{9,1},{17,9},{25,17},{10,2},{18,10},{26,18},{... | collective-permute-start | bytes 39944 | tf_op jit(solution)/shard_map/while/body/eval_jaxpr/ppermute | solution.py:14
  136.4 10.7 %collective-permute-start = (bf16[2,1,24,128]{3,2,1,0:T(8,128)(2,1)S(1)}, bf16[2,1,24,128]{3,2,1,0:T(8,128)(2,1)S(1)}, u32[]{:S(2)}, u32[]{:S(2)}) collective-permute-start(bf16[2,1,24,128]{3,2,1,0:T(8,128)(2,1)S(1)} %get-tuple-element.157), channel_id=1, source_target_pairs={{0,1},{1,2},{2,3},{3,4},{4,5},{5,6},{6,7},{8,9},{9,10},{10,11},{11... | collective-permute-start | bytes 36872 | tf_op jit(solution)/shard_map/while/body/eval_jaxpr/ppermute | solution.py:13
  141.5 5.7 %collective-permute-start.1 = (bf16[2,1,24,128]{3,2,1,0:T(8,128)(2,1)S(1)}, bf16[2,1,24,128]{3,2,1,0:T(8,128)(2,1)S(1)}, u32[]{:S(2)}, u32[]{:S(2)}) collective-permute-start(bf16[2,1,24,128]{3,2,1,0:T(8,128)(2,1)S(1)} %get-tuple-element.158), channel_id=1, source_target_pairs={{1,0},{2,1},{3,2},{4,3},{5,4},{6,5},{7,6},{9,8},{10,9},{11,10},{12... | collective-permute-start | bytes 36872 | tf_op jit(solution)/shard_map/while/body/eval_jaxpr/ppermute | solution.py:14
  150.5 4.6 %collective-permute-start.3 = (bf16[2,26,1,128]{3,2,1,0:T(2,128)(2,1)S(1)}, bf16[2,26,1,128]{3,2,1,0:T(2,128)(2,1)S(1)}, u32[]{:S(2)}, u32[]{:S(2)}) collective-permute-start(bf16[2,26,1,128]{3,2,1,0:T(2,128)(2,1)S(1)} %get-tuple-element.160), channel_id=1, source_target_pairs={{8,0},{16,8},{24,16},{9,1},{17,9},{25,17},{10,2},{18,10},{26,18},{... | collective-permute-start | bytes 39944 | tf_op jit(solution)/shard_map/while/body/eval_jaxpr/ppermute | solution.py:14
  160.1 10.7 %collective-permute-start = (bf16[2,1,24,128]{3,2,1,0:T(8,128)(2,1)S(1)}, bf16[2,1,24,128]{3,2,1,0:T(8,128)(2,1)S(1)}, u32[]{:S(2)}, u32[]{:S(2)}) collective-permute-start(bf16[2,1,24,128]{3,2,1,0:T(8,128)(2,1)S(1)} %get-tuple-element.157), channel_id=1, source_target_pairs={{0,1},{1,2},{2,3},{3,4},{4,5},{5,6},{6,7},{8,9},{9,10},{10,11},{11... | collective-permute-start | bytes 36872 | tf_op jit(solution)/shard_map/while/body/eval_jaxpr/ppermute | solution.py:13
  165.2 5.7 %collective-permute-start.1 = (bf16[2,1,24,128]{3,2,1,0:T(8,128)(2,1)S(1)}, bf16[2,1,24,128]{3,2,1,0:T(8,128)(2,1)S(1)}, u32[]{:S(2)}, u32[]{:S(2)}) collective-permute-start(bf16[2,1,24,128]{3,2,1,0:T(8,128)(2,1)S(1)} %get-tuple-element.158), channel_id=1, source_target_pairs={{1,0},{2,1},{3,2},{4,3},{5,4},{6,5},{7,6},{9,8},{10,9},{11,10},{12... | collective-permute-start | bytes 36872 | tf_op jit(solution)/shard_map/while/body/eval_jaxpr/ppermute | solution.py:14
  174.1 4.6 %collective-permute-start.3 = (bf16[2,26,1,128]{3,2,1,0:T(2,128)(2,1)S(1)}, bf16[2,26,1,128]{3,2,1,0:T(2,128)(2,1)S(1)}, u32[]{:S(2)}, u32[]{:S(2)}) collective-permute-start(bf16[2,26,1,128]{3,2,1,0:T(2,128)(2,1)S(1)} %get-tuple-element.160), channel_id=1, source_target_pairs={{8,0},{16,8},{24,16},{9,1},{17,9},{25,17},{10,2},{18,10},{26,18},{... | collective-permute-start | bytes 39944 | tf_op jit(solution)/shard_map/while/body/eval_jaxpr/ppermute | solution.py:14
  183.7 10.7 %collective-permute-start = (bf16[2,1,24,128]{3,2,1,0:T(8,128)(2,1)S(1)}, bf16[2,1,24,128]{3,2,1,0:T(8,128)(2,1)S(1)}, u32[]{:S(2)}, u32[]{:S(2)}) collective-permute-start(bf16[2,1,24,128]{3,2,1,0:T(8,128)(2,1)S(1)} %get-tuple-element.157), channel_id=1, source_target_pairs={{0,1},{1,2},{2,3},{3,4},{4,5},{5,6},{6,7},{8,9},{9,10},{10,11},{11... | collective-permute-start | bytes 36872 | tf_op jit(solution)/shard_map/while/body/eval_jaxpr/ppermute | solution.py:13
  188.8 5.7 %collective-permute-start.1 = (bf16[2,1,24,128]{3,2,1,0:T(8,128)(2,1)S(1)}, bf16[2,1,24,128]{3,2,1,0:T(8,128)(2,1)S(1)}, u32[]{:S(2)}, u32[]{:S(2)}) collective-permute-start(bf16[2,1,24,128]{3,2,1,0:T(8,128)(2,1)S(1)} %get-tuple-element.158), channel_id=1, source_target_pairs={{1,0},{2,1},{3,2},{4,3},{5,4},{6,5},{7,6},{9,8},{10,9},{11,10},{12... | collective-permute-start | bytes 36872 | tf_op jit(solution)/shard_map/while/body/eval_jaxpr/ppermute | solution.py:14
  194.6 4.5 %collective-permute-start.2 = (bf16[2,26,1,128]{3,2,1,0:T(2,128)(2,1)S(1)}, bf16[2,26,1,128]{3,2,1,0:T(2,128)(2,1)S(1)}, u32[]{:S(2)}, u32[]{:S(2)}) collective-permute-start(bf16[2,26,1,128]{3,2,1,0:T(2,128)(2,1)S(1)} %get-tuple-element.159), channel_id=1, source_target_pairs={{0,8},{8,16},{16,24},{1,9},{9,17},{17,25},{2,10},{10,18},{18,26},{... | collective-permute-start | bytes 39944 | tf_op jit(solution)/shard_map/while/body/eval_jaxpr/ppermute | solution.py:13
  197.8 4.6 %collective-permute-start.3 = (bf16[2,26,1,128]{3,2,1,0:T(2,128)(2,1)S(1)}, bf16[2,26,1,128]{3,2,1,0:T(2,128)(2,1)S(1)}, u32[]{:S(2)}, u32[]{:S(2)}) collective-permute-start(bf16[2,26,1,128]{3,2,1,0:T(2,128)(2,1)S(1)} %get-tuple-element.160), channel_id=1, source_target_pairs={{8,0},{16,8},{24,16},{9,1},{17,9},{25,17},{10,2},{18,10},{26,18},{... | collective-permute-start | bytes 39944 | tf_op jit(solution)/shard_map/while/body/eval_jaxpr/ppermute | solution.py:14
  207.4 10.7 %collective-permute-start = (bf16[2,1,24,128]{3,2,1,0:T(8,128)(2,1)S(1)}, bf16[2,1,24,128]{3,2,1,0:T(8,128)(2,1)S(1)}, u32[]{:S(2)}, u32[]{:S(2)}) collective-permute-start(bf16[2,1,24,128]{3,2,1,0:T(8,128)(2,1)S(1)} %get-tuple-element.157), channel_id=1, source_target_pairs={{0,1},{1,2},{2,3},{3,4},{4,5},{5,6},{6,7},{8,9},{9,10},{10,11},{11... | collective-permute-start | bytes 36872 | tf_op jit(solution)/shard_map/while/body/eval_jaxpr/ppermute | solution.py:13
  212.5 5.7 %collective-permute-start.1 = (bf16[2,1,24,128]{3,2,1,0:T(8,128)(2,1)S(1)}, bf16[2,1,24,128]{3,2,1,0:T(8,128)(2,1)S(1)}, u32[]{:S(2)}, u32[]{:S(2)}) collective-permute-start(bf16[2,1,24,128]{3,2,1,0:T(8,128)(2,1)S(1)} %get-tuple-element.158), channel_id=1, source_target_pairs={{1,0},{2,1},{3,2},{4,3},{5,4},{6,5},{7,6},{9,8},{10,9},{11,10},{12... | collective-permute-start | bytes 36872 | tf_op jit(solution)/shard_map/while/body/eval_jaxpr/ppermute | solution.py:14
  218.3 4.5 %collective-permute-start.2 = (bf16[2,26,1,128]{3,2,1,0:T(2,128)(2,1)S(1)}, bf16[2,26,1,128]{3,2,1,0:T(2,128)(2,1)S(1)}, u32[]{:S(2)}, u32[]{:S(2)}) collective-permute-start(bf16[2,26,1,128]{3,2,1,0:T(2,128)(2,1)S(1)} %get-tuple-element.159), channel_id=1, source_target_pairs={{0,8},{8,16},{16,24},{1,9},{9,17},{17,25},{2,10},{10,18},{18,26},{... | collective-permute-start | bytes 39944 | tf_op jit(solution)/shard_map/while/body/eval_jaxpr/ppermute | solution.py:13
  221.5 4.6 %collective-permute-start.3 = (bf16[2,26,1,128]{3,2,1,0:T(2,128)(2,1)S(1)}, bf16[2,26,1,128]{3,2,1,0:T(2,128)(2,1)S(1)}, u32[]{:S(2)}, u32[]{:S(2)}) collective-permute-start(bf16[2,26,1,128]{3,2,1,0:T(2,128)(2,1)S(1)} %get-tuple-element.160), channel_id=1, source_target_pairs={{8,0},{16,8},{24,16},{9,1},{17,9},{25,17},{10,2},{18,10},{26,18},{... | collective-permute-start | bytes 39944 | tf_op jit(solution)/shard_map/while/body/eval_jaxpr/ppermute | solution.py:14
  231.1 10.7 %collective-permute-start = (bf16[2,1,24,128]{3,2,1,0:T(8,128)(2,1)S(1)}, bf16[2,1,24,128]{3,2,1,0:T(8,128)(2,1)S(1)}, u32[]{:S(2)}, u32[]{:S(2)}) collective-permute-start(bf16[2,1,24,128]{3,2,1,0:T(8,128)(2,1)S(1)} %get-tuple-element.157), channel_id=1, source_target_pairs={{0,1},{1,2},{2,3},{3,4},{4,5},{5,6},{6,7},{8,9},{9,10},{10,11},{11... | collective-permute-start | bytes 36872 | tf_op jit(solution)/shard_map/while/body/eval_jaxpr/ppermute | solution.py:13
  236.2 5.7 %collective-permute-start.1 = (bf16[2,1,24,128]{3,2,1,0:T(8,128)(2,1)S(1)}, bf16[2,1,24,128]{3,2,1,0:T(8,128)(2,1)S(1)}, u32[]{:S(2)}, u32[]{:S(2)}) collective-permute-start(bf16[2,1,24,128]{3,2,1,0:T(8,128)(2,1)S(1)} %get-tuple-element.158), channel_id=1, source_target_pairs={{1,0},{2,1},{3,2},{4,3},{5,4},{6,5},{7,6},{9,8},{10,9},{11,10},{12... | collective-permute-start | bytes 36872 | tf_op jit(solution)/shard_map/while/body/eval_jaxpr/ppermute | solution.py:14
  241.9 4.5 %collective-permute-start.2 = (bf16[2,26,1,128]{3,2,1,0:T(2,128)(2,1)S(1)}, bf16[2,26,1,128]{3,2,1,0:T(2,128)(2,1)S(1)}, u32[]{:S(2)}, u32[]{:S(2)}) collective-permute-start(bf16[2,26,1,128]{3,2,1,0:T(2,128)(2,1)S(1)} %get-tuple-element.159), channel_id=1, source_target_pairs={{0,8},{8,16},{16,24},{1,9},{9,17},{17,25},{2,10},{10,18},{18,26},{... | collective-permute-start | bytes 39944 | tf_op jit(solution)/shard_map/while/body/eval_jaxpr/ppermute | solution.py:13
  245.1 4.6 %collective-permute-start.3 = (bf16[2,26,1,128]{3,2,1,0:T(2,128)(2,1)S(1)}, bf16[2,26,1,128]{3,2,1,0:T(2,128)(2,1)S(1)}, u32[]{:S(2)}, u32[]{:S(2)}) collective-permute-start(bf16[2,26,1,128]{3,2,1,0:T(2,128)(2,1)S(1)} %get-tuple-element.160), channel_id=1, source_target_pairs={{8,0},{16,8},{24,16},{9,1},{17,9},{25,17},{10,2},{18,10},{26,18},{... | collective-permute-start | bytes 39944 | tf_op jit(solution)/shard_map/while/body/eval_jaxpr/ppermute | solution.py:14
  254.8 10.7 %collective-permute-start = (bf16[2,1,24,128]{3,2,1,0:T(8,128)(2,1)S(1)}, bf16[2,1,24,128]{3,2,1,0:T(8,128)(2,1)S(1)}, u32[]{:S(2)}, u32[]{:S(2)}) collective-permute-start(bf16[2,1,24,128]{3,2,1,0:T(8,128)(2,1)S(1)} %get-tuple-element.157), channel_id=1, source_target_pairs={{0,1},{1,2},{2,3},{3,4},{4,5},{5,6},{6,7},{8,9},{9,10},{10,11},{11... | collective-permute-start | bytes 36872 | tf_op jit(solution)/shard_map/while/body/eval_jaxpr/ppermute | solution.py:13
  259.9 5.7 %collective-permute-start.1 = (bf16[2,1,24,128]{3,2,1,0:T(8,128)(2,1)S(1)}, bf16[2,1,24,128]{3,2,1,0:T(8,128)(2,1)S(1)}, u32[]{:S(2)}, u32[]{:S(2)}) collective-permute-start(bf16[2,1,24,128]{3,2,1,0:T(8,128)(2,1)S(1)} %get-tuple-element.158), channel_id=1, source_target_pairs={{1,0},{2,1},{3,2},{4,3},{5,4},{6,5},{7,6},{9,8},{10,9},{11,10},{12... | collective-permute-start | bytes 36872 | tf_op jit(solution)/shard_map/while/body/eval_jaxpr/ppermute | solution.py:14
  268.8 4.6 %collective-permute-start.3 = (bf16[2,26,1,128]{3,2,1,0:T(2,128)(2,1)S(1)}, bf16[2,26,1,128]{3,2,1,0:T(2,128)(2,1)S(1)}, u32[]{:S(2)}, u32[]{:S(2)}) collective-permute-start(bf16[2,26,1,128]{3,2,1,0:T(2,128)(2,1)S(1)} %get-tuple-element.160), channel_id=1, source_target_pairs={{8,0},{16,8},{24,16},{9,1},{17,9},{25,17},{10,2},{18,10},{26,18},{... | collective-permute-start | bytes 39944 | tf_op jit(solution)/shard_map/while/body/eval_jaxpr/ppermute | solution.py:14
  278.4 10.7 %collective-permute-start = (bf16[2,1,24,128]{3,2,1,0:T(8,128)(2,1)S(1)}, bf16[2,1,24,128]{3,2,1,0:T(8,128)(2,1)S(1)}, u32[]{:S(2)}, u32[]{:S(2)}) collective-permute-start(bf16[2,1,24,128]{3,2,1,0:T(8,128)(2,1)S(1)} %get-tuple-element.157), channel_id=1, source_target_pairs={{0,1},{1,2},{2,3},{3,4},{4,5},{5,6},{6,7},{8,9},{9,10},{10,11},{11... | collective-permute-start | bytes 36872 | tf_op jit(solution)/shard_map/while/body/eval_jaxpr/ppermute | solution.py:13
  283.5 5.7 %collective-permute-start.1 = (bf16[2,1,24,128]{3,2,1,0:T(8,128)(2,1)S(1)}, bf16[2,1,24,128]{3,2,1,0:T(8,128)(2,1)S(1)}, u32[]{:S(2)}, u32[]{:S(2)}) collective-permute-start(bf16[2,1,24,128]{3,2,1,0:T(8,128)(2,1)S(1)} %get-tuple-element.158), channel_id=1, source_target_pairs={{1,0},{2,1},{3,2},{4,3},{5,4},{6,5},{7,6},{9,8},{10,9},{11,10},{12... | collective-permute-start | bytes 36872 | tf_op jit(solution)/shard_map/while/body/eval_jaxpr/ppermute | solution.py:14
  292.5 4.6 %collective-permute-start.3 = (bf16[2,26,1,128]{3,2,1,0:T(2,128)(2,1)S(1)}, bf16[2,26,1,128]{3,2,1,0:T(2,128)(2,1)S(1)}, u32[]{:S(2)}, u32[]{:S(2)}) collective-permute-start(bf16[2,26,1,128]{3,2,1,0:T(2,128)(2,1)S(1)} %get-tuple-element.160), channel_id=1, source_target_pairs={{8,0},{16,8},{24,16},{9,1},{17,9},{25,17},{10,2},{18,10},{26,18},{... | collective-permute-start | bytes 39944 | tf_op jit(solution)/shard_map/while/body/eval_jaxpr/ppermute | solution.py:14
  302.1 10.7 %collective-permute-start = (bf16[2,1,24,128]{3,2,1,0:T(8,128)(2,1)S(1)}, bf16[2,1,24,128]{3,2,1,0:T(8,128)(2,1)S(1)}, u32[]{:S(2)}, u32[]{:S(2)}) collective-permute-start(bf16[2,1,24,128]{3,2,1,0:T(8,128)(2,1)S(1)} %get-tuple-element.157), channel_id=1, source_target_pairs={{0,1},{1,2},{2,3},{3,4},{4,5},{5,6},{6,7},{8,9},{9,10},{10,11},{11... | collective-permute-start | bytes 36872 | tf_op jit(solution)/shard_map/while/body/eval_jaxpr/ppermute | solution.py:13
  307.2 5.7 %collective-permute-start.1 = (bf16[2,1,24,128]{3,2,1,0:T(8,128)(2,1)S(1)}, bf16[2,1,24,128]{3,2,1,0:T(8,128)(2,1)S(1)}, u32[]{:S(2)}, u32[]{:S(2)}) collective-permute-start(bf16[2,1,24,128]{3,2,1,0:T(8,128)(2,1)S(1)} %get-tuple-element.158), channel_id=1, source_target_pairs={{1,0},{2,1},{3,2},{4,3},{5,4},{6,5},{7,6},{9,8},{10,9},{11,10},{12... | collective-permute-start | bytes 36872 | tf_op jit(solution)/shard_map/while/body/eval_jaxpr/ppermute | solution.py:14
  312.9 4.5 %collective-permute-start.2 = (bf16[2,26,1,128]{3,2,1,0:T(2,128)(2,1)S(1)}, bf16[2,26,1,128]{3,2,1,0:T(2,128)(2,1)S(1)}, u32[]{:S(2)}, u32[]{:S(2)}) collective-permute-start(bf16[2,26,1,128]{3,2,1,0:T(2,128)(2,1)S(1)} %get-tuple-element.159), channel_id=1, source_target_pairs={{0,8},{8,16},{16,24},{1,9},{9,17},{17,25},{2,10},{10,18},{18,26},{... | collective-permute-start | bytes 39944 | tf_op jit(solution)/shard_map/while/body/eval_jaxpr/ppermute | solution.py:13
  316.2 4.6 %collective-permute-start.3 = (bf16[2,26,1,128]{3,2,1,0:T(2,128)(2,1)S(1)}, bf16[2,26,1,128]{3,2,1,0:T(2,128)(2,1)S(1)}, u32[]{:S(2)}, u32[]{:S(2)}) collective-permute-start(bf16[2,26,1,128]{3,2,1,0:T(2,128)(2,1)S(1)} %get-tuple-element.160), channel_id=1, source_target_pairs={{8,0},{16,8},{24,16},{9,1},{17,9},{25,17},{10,2},{18,10},{26,18},{... | collective-permute-start | bytes 39944 | tf_op jit(solution)/shard_map/while/body/eval_jaxpr/ppermute | solution.py:14
  (46 other events, 166.6 us)
where the time goes:
time: 329 us; the launch traced here: 326 us
  starting transfers between devices  136 us (41%)
  local copies, waits for them, and re-layouts  61.2 us (19%)
  waiting for transfers between devices  49.1 us (15%)
  matrix products  39.7 us (12%)
  other arithmetic  37.6 us (11%)
    ppermute x26, starting transfers between devices, edge_swap(): from_prev = lax.ppermute(high_edge, axis_label, down_pairs)  93.2 us
    ppermute x26, waiting for transfers between devices, edge_swap(): from_next = lax.ppermute(low_edge, axis_label, up_pairs)  46.4 us
    ppermute x26, starting transfers between devices, edge_swap(): from_next = lax.ppermute(low_edge, axis_label, up_pairs)  42.4 us
    dot_general x24, matrix products, conv_taps(): jnp.dot(flat_patches, flat_weights, preferred_element_type=jnp.float32)  39.7 us
    concatenate x12, local copies, waits for them, and re-layouts, conv_taps(): patches = jnp.concatenate(tap_list, axis=-1)  26.8 us
    dynamic_update_slice x12, other arithmetic, local_run(): final_pair, all_hidden = lax.scan(step_fn, (h_init, c_init), frames_ext)  16.2 us
    squeeze x12, local copies, waits for them, and re-layouts, local_run(): final_pair, all_hidden = lax.scan(step_fn, (h_init, c_init), frames_ext)  12.5 us
    while x108, local copies, waits for them, and re-layouts  11.5 us
  transfers between devices with their start and end apart: 52, of which 16 were waited for; matrix products, arithmetic and copies ran while one was open for 20% of the time, Pallas kernels for 0%

commit v1 on v0

v1 whole, which is shorter than its diff:
```python
import jax
import jax.numpy as jnp
from jax import lax
from jax.experimental import pallas as pl
from jax.experimental.pallas import tpu as pltpu
from jax.sharding import PartitionSpec as P

BLOCK = 3
COL0 = 8
DIRS = ((-1, 0), (1, 0), (0, -1), (0, 1), (-1, -1), (-1, 1), (1, -1), (1, 1))
MESH = pl.DeviceIdType.MESH
F32 = jnp.float32
BF16 = jnp.bfloat16


def opposite(k):
    return DIRS.index((-DIRS[k][0], -DIRS[k][1]))


def make_kernel(steps, seqs, rows, cols, chan, hid, row_count, col_count):
    nblock = steps // BLOCK
    pitch = cols + 16
    hrows = rows + 2 * BLOCK + 6
    ring = BLOCK - 1
    xrow0 = 8
    nstrip = 2 * ring
    gates = 4 * hid
    kdim = 9 * hid + 3 * 128
    strip_cols = tuple(range(-ring, 0)) + tuple(range(cols, cols + ring))
    third = rows // 3

    def chunk_list(ext):
        own = [c for c in range(nstrip) if -ext <= strip_cols[c] < cols + ext]
        return (
            (-ext, third + ext, ()),
            (third, third, tuple(own)),
            (2 * third, third + ext, ()),
        )

    def kernel(frames, wx_ref, wh_hbm, bias_ref, hinit, cinit, hout, cout, *scratch):
        (hb0a, hb1a, hb2a, hb0b, hb1b, hb2b, xga, xgb, cma, cmb, csa, csb, xt, fbuf, wall,
         lhs0, lhs1, lhs2, gs0, gs1, gs2, ob, hin, sh, sc, sch, scc, rh, rc, rch, rcc, tmp, smask,
         lsem, osem, ssem, rsem, xssem, xrsem) = scratch
        hbs = ((hb0a, hb1a, hb2a), (hb0b, hb1b, hb2b))
        xgs = (xga, xgb)
        cms = (cma, cmb)
        css = (csa, csb)
        lhss = (lhs0, lhs1, lhs2)
        gss = (gs0, gs1, gs2)

        ri = lax.axis_index("rows")
        ci = lax.axis_index("cols")

        def exists(k):
            dr, dc = DIRS[k]
            conds = []
            if dr < 0:
                conds.append(ri > 0)
            if dr > 0:
                conds.append(ri < row_count - 1)
            if dc < 0:
                conds.append(ci > 0)
            if dc > 0:
                conds.append(ci < col_count - 1)
            out = conds[0]
            for extra in conds[1:]:
                out = jnp.logical_and(out, extra)
            return out

        def dev(k):
            return {"rows": ri + DIRS[k][0], "cols": ci + DIRS[k][1]}

        def h_addr(r, c):
            return (r + BLOCK) * pitch + COL0 + c

        def x_addr(r, c):
            return (r + ring) * pitch + COL0 + c

        cp_h = pltpu.make_async_copy(hinit, hin, lsem.at[0])
        cp_f = pltpu.make_async_copy(frames, fbuf, lsem.at[1])
        cp_w = pltpu.make_async_copy(wh_hbm, wall.at[pl.ds(0, 9 * hid), :], lsem.at[2])
        cp_c = [pltpu.make_async_copy(cinit.at[s], cms[s].at[pl.ds(ring * cols, rows * cols), :], lsem.at[3 + s]) for s in range(seqs)]
        cp_h.start()
        for s in range(seqs):
            cp_c[s].start()
        cp_f.start()
        cp_w.start()

        barrier = pltpu.get_barrier_semaphore()
        rh[...] = jnp.zeros_like(rh)
        rc[...] = jnp.zeros_like(rc)
        rch[...] = jnp.zeros_like(rch)
        rcc[...] = jnp.zeros_like(rcc)

        def zero_x(i, _):
            xt[i] = jnp.zeros(xt.shape[1:], F32)
            return 0

        lax.fori_loop(0, steps * seqs, zero_x, 0)
        for k in range(8):
            @pl.when(exists(k))
            def _():
                pl.semaphore_signal(barrier, 1, device_id=dev(k), device_id_type=MESH)
        for s in range(seqs):
            for q in range(3):
                hbs[s][q][...] = jnp.zeros_like(hbs[s][q])
            css[s][...] = jnp.zeros_like(css[s])
            cms[s][pl.ds(0, ring * cols), :] = jnp.zeros((ring * cols, hid), F32)
            cms[s][pl.ds((rows + ring) * cols, ring * cols), :] = jnp.zeros((ring * cols, hid), F32)
            xgs[s][...] = jnp.zeros_like(xgs[s])

        top_ok = jnp.where(ri > 0, 1.0, 0.0).astype(F32)
        bot_ok = jnp.where(ri < row_count - 1, 1.0, 0.0).astype(F32)
        left_ok = jnp.where(ci > 0, 1.0, 0.0).astype(F32)
        right_ok = jnp.where(ci < col_count - 1, 1.0, 0.0).astype(F32)
        srow = lax.broadcasted_iota(jnp.int32, (32, hid), 0)
        rmask = jnp.where(srow < ring, top_ok, jnp.where(srow >= rows + ring, bot_ok, 1.0))
        smask[0] = rmask * left_ok
        smask[1] = rmask * right_ok

        n_row = jnp.where(ri > 0, 1, 0) + jnp.where(ri < row_count - 1, 1, 0)
        n_col = jnp.where(ci > 0, 1, 0) + jnp.where(ci < col_count - 1, 1, 0)
        pl.semaphore_wait(barrier, (n_row + 1) * (n_col + 1) - 1)

        def msg_copies(s, k, par):
            if k < 4:
                pairs = ((sh.at[s, k], rh.at[par, s, k]), (sc.at[s, k], rc.at[par, s, k]))
            else:
                pairs = ((sch.at[s, k - 4], rch.at[par, s, k - 4]), (scc.at[s, k - 4], rcc.at[par, s, k - 4]))
            return [
                pltpu.make_async_remote_copy(src_ref=a, dst_ref=b, send_sem=ssem.at[s, k, n], recv_sem=rsem.at[par, s, k, n], device_id=dev(k), device_id_type=MESH)
                for n, (a, b) in enumerate(pairs)
            ]

        def pack(s):
            hb = hbs[s][0]
            cm = cms[s]
            for k in range(8):
                dr, dc = DIRS[k]
                r0 = 0 if dr < 0 else rows - BLOCK
                rc0 = 0 if dr < 0 else rows - ring
                c0 = 0 if dc < 0 else cols - BLOCK
                cc0 = 0 if dc < 0 else cols - ring
                if dc == 0:
                    v = jnp.concatenate([hb[pl.ds(h_addr(r0 + i, 0), cols), :] for i in range(BLOCK)], axis=0)
                    sh[s, k, pl.ds(0, BLOCK * cols), :] = v.astype(BF16)
                    sc[s, k] = cm[pl.ds((rc0 + ring) * cols, ring * cols), :]
                elif dr == 0:
                    v = jnp.concatenate([hb[pl.ds(h_addr(0, c0 + j), rows, stride=pitch), :] for j in range(BLOCK)], axis=0)
                    sh[s, k, pl.ds(0, BLOCK * rows), :] = v.astype(BF16)
                    for j in range(ring):
                        sc[s, k, pl.ds(j * rows, rows), :] = cm[pl.ds(ring * cols + cc0 + j, rows, stride=cols), :]
                else:
                    for i in range(BLOCK):
                        tmp[pl.ds(i * BLOCK, BLOCK), :] = hb[pl.ds(h_addr(r0 + i, c0), BLOCK), :]
                    sch[s, k - 4] = tmp[pl.ds(0, 16), :].astype(BF16)
                    for j in range(ring):
                        scc[s, k - 4, pl.ds(j * ring, ring), :] = cm[pl.ds((rc0 + ring) * cols + cc0 + j, ring, stride=cols), :]

        def unpack(s, par):
            hb = hbs[s][0]
            cm = cms[s]
            cs = css[s]
            for k in range(8):
                dr, dc = DIRS[k]
                o = opposite(k)
                r0 = -BLOCK if dr < 0 else rows
                c0 = -BLOCK if dc < 0 else cols
                st0 = 0 if dc < 0 else ring
                q0 = 0 if dr < 0 else rows + ring
                if dc == 0:
                    v = rh[par, s, o, pl.ds(0, BLOCK * cols), :].astype(F32)
                    for i in range(BLOCK):
                        hb[pl.ds(h_addr(r0 + i, 0), cols), :] = v[i * cols:(i + 1) * cols]
                    cm[pl.ds(q0 * cols, ring * cols), :] = rc[par, s, o]
                elif dr == 0:
                    v = rh[par, s, o, pl.ds(0, BLOCK * rows), :].astype(F32)
                    for j in range(BLOCK):
                        hb[pl.ds(h_addr(0, c0 + j), rows, stride=pitch), :] = v[j * rows:(j + 1) * rows]
                    for j in range(ring):
                        cs[pl.ds((st0 + j) * 32 + ring, rows), :] = rc[par, s, o, pl.ds(j * rows, rows), :]
                else:
                    tmp[pl.ds(0, 16), :] = rch[par, s, o - 4].astype(F32)
                    for i in range(BLOCK):
                        hb[pl.ds(h_addr(r0 + i, c0), BLOCK), :] = tmp[pl.ds(i * BLOCK, BLOCK), :]
                    for j in range(ring):
                        cs[pl.ds((st0 + j) * 32 + q0, ring), :] = rcc[par, s, o - 4, pl.ds(j * ring, ring), :]

        def send(s, par):
            for k in range(8):
                @pl.when(exists(k))
                def _():
                    for cp in msg_copies(s, k, par):
                        cp.start()

        def wait_send(s):
            for k in range(8):
                @pl.when(exists(k))
                def _():
                    for cp in msg_copies(s, k, 0):
                        cp.wait_send()

        def wait_recv(s, par):
            for k in range(8):
                @pl.when(exists(k))
                def _():
                    for cp in msg_copies(s, opposite(k), par):
                        cp.wait_recv()

        own_lane = xrow0 * chan
        row_lanes = rows * chan

        def x_copy(t, k):
            dr, dc = DIRS[k]
            if dr == 0:
                lanes_s, lanes_d, lane_n = own_lane, own_lane, row_lanes
            else:
                lane_n = 8 * chan
                lanes_s = own_lane if dr < 0 else own_lane + row_lanes - lane_n
                lanes_d = own_lane + row_lanes if dr < 0 else 0
            if dc == 0:
                sub_s, sub_d, sub_n = COL0, COL0, cols
            else:
                sub_n = 8
                sub_s = COL0 if dc < 0 else COL0 + cols - 8
                sub_d = COL0 + cols if dc < 0 else 0
            return pltpu.make_async_remote_copy(
                src_ref=xt.at[pl.ds(t * seqs, seqs), pl.ds(sub_s, sub_n), pl.ds(lanes_s, lane_n)],
                dst_ref=xt.at[pl.ds(t * seqs, seqs), pl.ds(sub_d, sub_n), pl.ds(lanes_d, lane_n)],
                send_sem=xssem.at[t, k], recv_sem=xrsem.at[t, k], device_id=dev(k), device_id_type=MESH)

        cp_h.wait()
        for s in range(seqs):
            for r in range(0, rows, 2):
                v = hin[s, pl.ds(r * cols, 2 * cols), :].astype(F32)
                for i in range(2):
                    hbs[s][0][pl.ds(h_addr(r + i, 0), cols), :] = v[i * cols:(i + 1) * cols]
            cp_c[s].wait()
            pack(s)
            send(s, 0)

        eye = (lax.broadcasted_iota(jnp.int32, (cols, cols), 0) == lax.broadcasted_iota(jnp.int32, (cols, cols), 1)).astype(F32).astype(BF16)
        cp_f.wait()

        def prep_x(t, _):
            for s in range(seqs):
                xt[t * seqs + s, pl.ds(COL0, cols), pl.ds(own_lane, row_lanes)] = lax.dot_general(
                    eye, fbuf[t * seqs + s], (((1,), (1,)), ((), ())), preferred_element_type=F32)
            for k in range(8):
                @pl.when(exists(k))
                def _():
                    x_copy(t, k).start()
            return 0

        lax.fori_loop(0, steps, prep_x, 0)

        cp_w.wait()
        wall[pl.ds(9 * hid, 3 * 128), :] = jnp.zeros((3 * 128, gates), BF16)
        for dc in range(3):
            for dr in range(3):
                wall[pl.ds(9 * hid + dc * 128 + dr * chan, chan), :] = wx_ref[dr, dc]

        lane = lax.broadcasted_iota(jnp.int32, (pitch, 128), 1)

        def build_xg(s, t, ext):
            xg = xgs[s]
            for r in range(-ext, rows + ext):
                start = r - 1 + xrow0
                g, off = divmod(start, 8)
                v = xt[t * seqs + s, :, pl.ds(g * 128, 128)]
                if off:
                    v = pltpu.roll(v, 128 - chan * off, 1)
                    if off > 5:
                        w = pltpu.roll(xt[t * seqs + s, :, pl.ds((g + 1) * 128, 128)], 128 - chan * off, 1)
                        v = jnp.where(lane < 128 - chan * off, v, w)
                xg[pl.ds(x_addr(r, -COL0), pitch), :] = v

        def build_lhs(s, j, ch):
            hb = hbs[s][j]
            xg = xgs[s]
            r0, nr, strips = chunk_list(BLOCK - 1 - j)[ch]
            lhs = lhss[ch]
            base = 32 * len(strips)
            for tap in range(12):
                for n, k in enumerate(strips):
                    if tap < 9:
                        dr, dc = tap // 3 - 1, tap % 3 - 1
                        v = hb[pl.ds(h_addr(-ring + dr, strip_cols[k] + dc), 32, stride=pitch), :]
                    else:
                        v = xg[pl.ds(x_addr(-ring, strip_cols[k] + tap - 10), 32, stride=pitch), :]
                    lhs[pl.ds(32 * n, 32), pl.ds(tap * 128, 128)] = v.astype(BF16)
                for i in range(0, nr, 2):
                    pieces = []
                    for r in range(r0 + i, min(r0 + i + 2, r0 + nr)):
                        if tap < 9:
                            dr, dc = tap // 3 - 1, tap % 3 - 1
                            pieces.append(hb[pl.ds(h_addr(r + dr, dc), cols), :])
                        else:
                            pieces.append(xg[pl.ds(x_addr(r, tap - 10), cols), :])
                    v = jnp.concatenate(pieces, axis=0) if len(pieces) > 1 else pieces[0]
                    lhs[pl.ds(base + i * cols, len(pieces) * cols), pl.ds(tap * 128, 128)] = v.astype(BF16)

        def matmul(j, ch):
            r0, nr, strips = chunk_list(BLOCK - 1 - j)[ch]
            m = -(-(32 * len(strips) + nr * cols) // 16) * 16
            gss[ch][pl.ds(0, m), :] = jnp.dot(lhss[ch][pl.ds(0, m), :], wall[...], preferred_element_type=F32)

        def cell(g_ref, m0, n, c):
            b = bias_ref[...]
            acts = []
            for q in range(4):
                g = g_ref[pl.ds(m0, n), pl.ds(q * hid, hid)] + b[:, q * hid:(q + 1) * hid]
                acts.append(jnp.tanh(g) if q == 3 else 0.5 * jnp.tanh(0.5 * g) + 0.5)
            c_new = acts[1] * c + acts[0] * acts[3]
            return acts[2] * jnp.tanh(c_new), c_new

        def elementwise(s, j, ch):
            ext = BLOCK - 1 - j
            dst = hbs[s][(j + 1) % BLOCK]
            r0, nr, strips = chunk_list(ext)[ch]
            base = 32 * len(strips)
            for n, k in enumerate(strips):
                h, c_new = cell(gss[ch], 32 * n, 32, css[s][pl.ds(32 * k, 32), :])
                css[s][pl.ds(32 * k, 32), :] = c_new
                h = h * smask[0 if strip_cols[k] < 0 else 1]
                dst[pl.ds(h_addr(-ring, strip_cols[k]), 32, stride=pitch), :] = h.astype(BF16).astype(F32)
            r = r0
            while r < r0 + nr:
                inside = 0 <= r < rows
                cnt = 2 if inside else 1
                crow = (r + ring) * cols
                h, c_new = cell(gss[ch], base + (r - r0) * cols, cnt * cols, cms[s][pl.ds(crow, cnt * cols), :])
                cms[s][pl.ds(crow, cnt * cols), :] = c_new
                if not inside:
                    h = h * (top_ok if r < 0 else bot_ok)
                hb16 = h.astype(BF16)
                if inside:
                    ob[s, j, pl.ds(r * cols, cnt * cols), :] = hb16
                h = hb16.astype(F32)
                for i in range(cnt):
                    dst[pl.ds(h_addr(r + i, 0), cols), :] = h[i * cols:(i + 1) * cols]
                r += cnt

        def out_copy(s, j, b):
            return pltpu.make_async_copy(ob.at[s, j], hout.at[b * BLOCK + j, s], osem.at[s, j])

        def block(b, _):
            par = lax.rem(b, 2)
            for s in range(seqs):
                wait_recv(s, par)
                if s == 0:
                    for j in range(BLOCK):
                        for k in range(8):
                            @pl.when(exists(k))
                            def _():
                                x_copy(b * BLOCK + j, opposite(k)).wait_recv()

                @pl.when(b > 0)
                def _():
                    for j in range(BLOCK):
                        out_copy(s, j, b - 1).wait()

                unpack(s, par)
                late = None
                for j in range(BLOCK):
                    build_xg(s, b * BLOCK + j, BLOCK - 1 - j)
                    for ch in range(3):
                        build_lhs(s, j, ch)
                        matmul(j, ch)
                        if late is not None:
                            elementwise(s, *late)
                        late = (j, ch)
                elementwise(s, *late)
                wait_send(s)

                @pl.when(b < nblock - 1)
                def _():
                    pack(s)
                    send(s, 1 - par)

                for j in range(BLOCK):
                    out_copy(s, j, b).start()
            return 0

        lax.fori_loop(0, nblock, block, 0)

        fin = [pltpu.make_async_copy(cms[s].at[pl.ds(ring * cols, rows * cols), :], cout.at[s], lsem.at[3 + s]) for s in range(seqs)]
        for cp in fin:
            cp.start()
        for t in range(steps):
            for k in range(8):
                @pl.when(exists(k))
                def _():
                    x_copy(t, k).wait_send()
        for s in range(seqs):
            for j in range(BLOCK):
                out_copy(s, j, nblock - 1).wait()
        for cp in fin:
            cp.wait()

    hbuf = pltpu.VMEM((hrows * pitch, hid), F32)
    xbuf = pltpu.VMEM((hrows * pitch, 128), F32)
    mmax = [-(-max(32 * len(chunk_list(e)[ch][2]) + chunk_list(e)[ch][1] * cols for e in range(BLOCK)) // 16) * 16 for ch in range(3)]
    scratch = (
        [hbuf] * 6 + [xbuf] * 2
        + [pltpu.VMEM(((rows + 2 * ring) * cols, hid), F32)] * 2
        + [pltpu.VMEM((nstrip * 32, hid), F32)] * 2
        + [
            pltpu.VMEM((steps * seqs, pitch, (rows + 16) * chan), F32),
            pltpu.VMEM((steps * seqs, rows * chan, cols), BF16),
            pltpu.VMEM((kdim, gates), BF16),
        ]
        + [pltpu.VMEM((mmax[ch], kdim), BF16) for ch in range(3)]
        + [pltpu.VMEM((mmax[ch], gates), F32) for ch in range(3)]
        + [
            pltpu.VMEM((seqs, BLOCK, rows * cols, hid), BF16),
            pltpu.VMEM((seqs, rows * cols, hid), BF16),
            pltpu.VMEM((seqs, 4, 80, hid), BF16),
            pltpu.VMEM((seqs, 4, ring * cols, hid), F32),
            pltpu.VMEM((seqs, 4, 16, hid), BF16),
            pltpu.VMEM((seqs, 4, 8, hid), F32),
            pltpu.VMEM((2, seqs, 4, 80, hid), BF16),
            pltpu.VMEM((2, seqs, 4, ring * cols, hid), F32),
            pltpu.VMEM((2, seqs, 4, 16, hid), BF16),
            pltpu.VMEM((2, seqs, 4, 8, hid), F32),
            pltpu.VMEM((16, hid), F32),
            pltpu.VMEM((2, 32, hid), F32),
            pltpu.SemaphoreType.DMA((5,)),
            pltpu.SemaphoreType.DMA((seqs, BLOCK)),
            pltpu.SemaphoreType.DMA((seqs, 8, 2)),
            pltpu.SemaphoreType.DMA((2, seqs, 8, 2)),
            pltpu.SemaphoreType.DMA((steps, 8)),
            pltpu.SemaphoreType.DMA((steps, 8)),
        ]
    )
    return kernel, scratch


def solution(mesh):
    row_count = mesh.shape["rows"]
    col_count = mesh.shape["cols"]
    frame_spec = P(None, "batch", "rows", "cols", None)
    state_spec = P("batch", "rows", "cols", None)

    def local_run(frames, w_x, w_h, gate_bias, h_init, c_init):
        steps, seqs, rows, cols, chan = frames.shape
        hid = h_init.shape[-1]
        gates = 4 * hid
        kernel, scratch = make_kernel(steps, seqs, rows, cols, chan, hid, row_count, col_count)
        anyspace = pl.BlockSpec(memory_space=pl.ANY)
        vmem = pl.BlockSpec(memory_space=pltpu.VMEM)
        ft = frames.transpose(0, 1, 2, 4, 3).reshape(steps * seqs, rows * chan, cols)
        all_hidden, cell_last = pl.pallas_call(
            kernel,
            out_shape=(
                jax.ShapeDtypeStruct((steps, seqs, rows * cols, hid), BF16),
                jax.ShapeDtypeStruct((seqs, rows * cols, hid), F32),
            ),
            in_specs=[anyspace, vmem, anyspace, vmem, anyspace, anyspace],
            out_specs=(anyspace, anyspace),
            scratch_shapes=scratch,
            compiler_params=pltpu.CompilerParams(collective_id=0, has_side_effects=True, vmem_limit_bytes=60 * 1024 * 1024),
        )(
            ft, w_x, w_h.reshape(9 * hid, gates), gate_bias.reshape(1, gates),
            h_init.reshape(seqs, rows * cols, hid), c_init.reshape(seqs, rows * cols, hid),
        )
        return all_hidden.reshape(steps, seqs, rows, cols, hid), cell_last.reshape(seqs, rows, cols, hid)

    return jax.shard_map(local_run, mesh=mesh, in_specs=(frame_spec, P(), P(), P(), state_spec, state_spec), out_specs=(frame_spec, state_spec), check_vma=False)
```

time: 329 us -> 61.6 us (0.19)
  starting transfers between devices: 136 us -> 0 us
  local copies, waits for them, and re-layouts: 61.2 us -> 5.31 us
  Pallas kernels: 0 us -> 55.5 us
  waiting for transfers between devices: 49.1 us -> 0 us
  matrix products: 39.7 us -> 0 us
  other arithmetic: 37.6 us -> 0 us
    ppermute x52 -> x0, starting transfers between devices: 136 us -> none  [the longest x26 93.2 us: edge_swap(): from_prev = lax.ppermute(high_edge, axis_label, down_pairs)]
    pallas_call x0 -> x1, Pallas kernels: none -> 55.5 us  [local_run(): pl.pallas_call(kernel, out_shape=(jax.ShapeDtypeStruct((steps, seqs, rows...]
    ppermute x52 -> x0, waiting for transfers between devices: 49.1 us -> none  [the longest x26 46.4 us: edge_swap(): from_next = lax.ppermute(low_edge, axis_label, up_pairs)]
    dot_general x24 -> x0, matrix products: 39.7 us -> none  [conv_taps(): jnp.dot(flat_patches, flat_weights, preferred_element_type=jnp.float32)]
    concatenate x24 -> x0, local copies, waits for them, and re-layouts: 27 us -> none  [the longest x12 26.8 us: conv_taps(): patches = jnp.concatenate(tap_list, axis=-1)]
    dynamic_update_slice x12 -> x0, other arithmetic: 16.2 us -> none  [local_run(): final_pair, all_hidden = lax.scan(step_fn, (h_init, c_init), frames_ext)]
    squeeze x12 -> x0, local copies, waits for them, and re-layouts: 12.5 us -> none  [local_run(): final_pair, all_hidden = lax.scan(step_fn, (h_init, c_init), frames_ext)]
    while x108 -> x0, local copies, waits for them, and re-layouts: 11.5 us -> none
  transfers between devices with their start and end apart: 52 -> 0, of which waited for: 16 -> 0; matrix products, arithmetic and copies ran while one was open for 20% -> 0% of each run, Pallas kernels for 0% -> 0%
where the time goes in v1:
time: 61.6 us; the launch traced here: 61.5 us
  Pallas kernels  55.5 us (90%)
  local copies, waits for them, and re-layouts  5.31 us (9%)
  between operations  0.65 us (1%)
    pallas_call x1, Pallas kernels, local_run(): pl.pallas_call(kernel, out_shape=(jax.ShapeDtypeStruct((steps, seqs, rows...  55.5 us
    unnamed x4, local copies, waits for them, and re-layouts  5.31 us

profile of v1, /device:TPU:97, one launch (start us, length us, event | category | flops | bytes accessed | tf_op | source)
XLA Modules:
  0.0 61.5 jit_solution(10130885575804075621)
XLA Ops:
  0.6 55.5 %shard_map.77 = (bf16[12,2,576,128]{3,2,1,0:T(8,128)(2,1)}, f32[2,576,128]{2,1,0:T(8,128)}) custom-call(bf16[24,384,24]{2,1,0:T(8,128)(2,1)} %bitcast.10, bf16[3,3,16,512]{3,2,1,0:T(8,128)(2,1)} %wx_ref.1, bf16[1152,512]{1,0:T(8,128)(2,1)} %bitcast.11, f32[1,512]{1,0:T(1,128)} %bitcast.15, bf16[2,576,128]{2,1,0:T(8,128)(2,1)} %bitcast.14, ...), custom_call_target="tpu_custom_call" | custom-call | tf_op jit(solution)/shard_map/pallas_call | solution.py:453
  56.2 0.0 copy-start
  56.2 4.5 %copy.10 = bf16[12,2,24,24,128]{4,3,2,1,0:T(8,128)(2,1)} copy(bf16[12,2,24,24,128]{4,3,2,1,0:T(8,128)(2,1)} %bitcast.9) | data formatting | bytes 7077888
  60.7 0.0 copy-done
  60.7 0.8 %copy.11 = f32[2,24,24,128]{3,2,1,0:T(8,128)} copy(f32[2,24,24,128]{3,2,1,0:T(8,128)S(1)} %bitcast.12) | data formatting | bytes 1179648
Async XLA Ops:
  56.2 4.5 %copy-start = (f32[2,576,128]{2,1,0:T(8,128)S(1)}, f32[2,576,128]{2,1,0:T(8,128)}, u32[]{:S(2)}) copy-start(f32[2,576,128]{2,1,0:T(8,128)} %get-tuple-element.5) | copy-start | bytes 1769476

commit v2 on v1

--- a/solution.py
+++ b/solution.py
@@ -37,10 +37,10 @@
             (2 * third, third + ext, ()),
         )
 
-    def kernel(frames, wx_ref, wh_hbm, bias_ref, hinit, cinit, hout, cout, *scratch):
+    def kernel(frames, wx_hbm, wh_hbm, bias_hbm, hinit, cinit, hout, cout, *scratch):
         (hb0a, hb1a, hb2a, hb0b, hb1b, hb2b, xga, xgb, cma, cmb, csa, csb, xt, fbuf, wall,
-         lhs0, lhs1, lhs2, gs0, gs1, gs2, ob, hin, sh, sc, sch, scc, rh, rc, rch, rcc, tmp, smask,
-         lsem, osem, ssem, rsem, xssem, xrsem) = scratch
+         lhs0, lhs1, lhs2, gs0, gs1, gs2, wx_ref, bias_ref, hin, sh, sc, sch, scc, rh, rc, rch, rcc, tmp, smask,
+         lsem, ssem, rsem, xssem, xrsem) = scratch
         hbs = ((hb0a, hb1a, hb2a), (hb0b, hb1b, hb2b))
         xgs = (xga, xgb)
         cms = (cma, cmb)
@@ -77,14 +77,21 @@
             return (r + ring) * pitch + COL0 + c
 
         cp_h = pltpu.make_async_copy(hinit, hin, lsem.at[0])
-        cp_f = pltpu.make_async_copy(frames, fbuf, lsem.at[1])
+        near = BLOCK * seqs
+        far = steps * seqs - near
+        cp_f = pltpu.make_async_copy(frames.at[pl.ds(0, near)], fbuf.at[pl.ds(0, near)], lsem.at[1])
+        cp_g = pltpu.make_async_copy(frames.at[pl.ds(near, far)], fbuf.at[pl.ds(near, far)], lsem.at[5])
         cp_w = pltpu.make_async_copy(wh_hbm, wall.at[pl.ds(0, 9 * hid), :], lsem.at[2])
         cp_c = [pltpu.make_async_copy(cinit.at[s], cms[s].at[pl.ds(ring * cols, rows * cols), :], lsem.at[3 + s]) for s in range(seqs)]
+        cp_small = [pltpu.make_async_copy(wx_hbm, wx_ref, lsem.at[6]), pltpu.make_async_copy(bias_hbm, bias_ref, lsem.at[7])]
         cp_h.start()
         for s in range(seqs):
             cp_c[s].start()
         cp_f.start()
         cp_w.start()
+        for cp in cp_small:
+            cp.start()
+        cp_g.start()
 
         barrier = pltpu.get_barrier_semaphore()
         rh[...] = jnp.zeros_like(rh)
@@ -92,8 +99,13 @@
         rch[...] = jnp.zeros_like(rch)
         rcc[...] = jnp.zeros_like(rcc)
 
+        xlanes = xt.shape[2]
+
         def zero_x(i, _):
-            xt[i] = jnp.zeros(xt.shape[1:], F32)
+            for sub in (0, COL0 + cols):
+                xt[i, pl.ds(sub, 8), :] = jnp.zeros((8, xlanes), F32)
+            for lane0 in (0, xlanes - 128):
+                xt[i, pl.ds(COL0, cols), pl.ds(lane0, 128)] = jnp.zeros((cols, 128), F32)
             return 0
 
         lax.fori_loop(0, steps * seqs, zero_x, 0)
@@ -101,14 +113,6 @@
             @pl.when(exists(k))
             def _():
                 pl.semaphore_signal(barrier, 1, device_id=dev(k), device_id_type=MESH)
-        for s in range(seqs):
-            for q in range(3):
-                hbs[s][q][...] = jnp.zeros_like(hbs[s][q])
-            css[s][...] = jnp.zeros_like(css[s])
-            cms[s][pl.ds(0, ring * cols), :] = jnp.zeros((ring * cols, hid), F32)
-            cms[s][pl.ds((rows + ring) * cols, ring * cols), :] = jnp.zeros((ring * cols, hid), F32)
-            xgs[s][...] = jnp.zeros_like(xgs[s])
-
         top_ok = jnp.where(ri > 0, 1.0, 0.0).astype(F32)
         bot_ok = jnp.where(ri < row_count - 1, 1.0, 0.0).astype(F32)
         left_ok = jnp.where(ci > 0, 1.0, 0.0).astype(F32)
@@ -128,7 +132,7 @@
             else:
                 pairs = ((sch.at[s, k - 4], rch.at[par, s, k - 4]), (scc.at[s, k - 4], rcc.at[par, s, k - 4]))
             return [
-                pltpu.make_async_remote_copy(src_ref=a, dst_ref=b, send_sem=ssem.at[s, k, n], recv_sem=rsem.at[par, s, k, n], device_id=dev(k), device_id_type=MESH)
+                pltpu.make_async_remote_copy(src_ref=a, dst_ref=b, send_sem=ssem.at[s], recv_sem=rsem.at[par, s], device_id=dev(k), device_id_type=MESH)
                 for n, (a, b) in enumerate(pairs)
             ]
 
@@ -186,26 +190,25 @@
                     for j in range(ring):
                         cs[pl.ds((st0 + j) * 32 + q0, ring), :] = rcc[par, s, o - 4, pl.ds(j * ring, ring), :]
 
-        def send(s, par):
+        def send(s, par, more=None):
             for k in range(8):
-                @pl.when(exists(k))
+                @pl.when(exists(k) if more is None else jnp.logical_and(exists(k), more))
                 def _():
                     for cp in msg_copies(s, k, par):
                         cp.start()
 
-        def wait_send(s):
-            for k in range(8):
-                @pl.when(exists(k))
-                def _():
-                    for cp in msg_copies(s, k, 0):
-                        cp.wait_send()
-
-        def wait_recv(s, par):
-            for k in range(8):
-                @pl.when(exists(k))
-                def _():
-                    for cp in msg_copies(s, opposite(k), par):
-                        cp.wait_recv()
+        def wait_all(sem, side, corner, more=None):
+            for a in ((1, 2) if row_count > 2 else (row_count - 1,)):
+                for b in ((1, 2) if col_count > 2 else (col_count - 1,)):
+                    n = side * (a + b) + corner * a * b
+                    cond = jnp.logical_and(n_row == a, n_col == b)
+
+                    @pl.when(cond if more is None else jnp.logical_and(cond, more))
+                    def _():
+                        pltpu.make_async_copy(cinit.at[0, pl.ds(0, n)], cma.at[pl.ds(0, n)], sem).wait()
+
+        msg_side, msg_corner = 40 + ring * cols, 16
+        x_side, x_corner = seqs * cols, seqs * 8
 
         own_lane = xrow0 * chan
         row_lanes = rows * chan
@@ -227,34 +230,45 @@
             return pltpu.make_async_remote_copy(
                 src_ref=xt.at[pl.ds(t * seqs, seqs), pl.ds(sub_s, sub_n), pl.ds(lanes_s, lane_n)],
                 dst_ref=xt.at[pl.ds(t * seqs, seqs), pl.ds(sub_d, sub_n), pl.ds(lanes_d, lane_n)],
-                send_sem=xssem.at[t, k], recv_sem=xrsem.at[t, k], device_id=dev(k), device_id_type=MESH)
-
-        cp_h.wait()
-        for s in range(seqs):
+                send_sem=xssem.at[lax.rem(t, BLOCK)], recv_sem=xrsem.at[lax.rem(lax.div(t, BLOCK), 2), lax.rem(t, BLOCK)], device_id=dev(k), device_id_type=MESH)
+
+        def load_state(s):
             for r in range(0, rows, 2):
                 v = hin[s, pl.ds(r * cols, 2 * cols), :].astype(F32)
                 for i in range(2):
                     hbs[s][0][pl.ds(h_addr(r + i, 0), cols), :] = v[i * cols:(i + 1) * cols]
-            cp_c[s].wait()
-            pack(s)
-            send(s, 0)
+
+        cp_h.wait()
+        load_state(0)
+        cp_c[0].wait()
+        pack(0)
+        send(0, 0)
 
         eye = (lax.broadcasted_iota(jnp.int32, (cols, cols), 0) == lax.broadcasted_iota(jnp.int32, (cols, cols), 1)).astype(F32).astype(BF16)
-        cp_f.wait()
-
-        def prep_x(t, _):
+
+        def prep_x(t):
             for s in range(seqs):
                 xt[t * seqs + s, pl.ds(COL0, cols), pl.ds(own_lane, row_lanes)] = lax.dot_general(
                     eye, fbuf[t * seqs + s], (((1,), (1,)), ((), ())), preferred_element_type=F32)
+
+        def send_x(t, more=None):
             for k in range(8):
-                @pl.when(exists(k))
+                @pl.when(exists(k) if more is None else jnp.logical_and(exists(k), more))
                 def _():
                     x_copy(t, k).start()
-            return 0
-
-        lax.fori_loop(0, steps, prep_x, 0)
+
+        cp_f.wait()
+        for t in range(BLOCK):
+            prep_x(t)
+        for t in range(BLOCK):
+            send_x(t)
+        load_state(1)
+        cp_c[1].wait()
+        cp_g.wait()
 
         cp_w.wait()
+        for cp in cp_small:
+            cp.wait()
         wall[pl.ds(9 * hid, 3 * 128), :] = jnp.zeros((3 * 128, gates), BF16)
         for dc in range(3):
             for dr in range(3):
@@ -314,7 +328,7 @@
             c_new = acts[1] * c + acts[0] * acts[3]
             return acts[2] * jnp.tanh(c_new), c_new
 
-        def elementwise(s, j, ch):
+        def elementwise(s, j, ch, t, skip=None):
             ext = BLOCK - 1 - j
             dst = hbs[s][(j + 1) % BLOCK]
             r0, nr, strips = chunk_list(ext)[ch]
@@ -329,74 +343,72 @@
                 inside = 0 <= r < rows
                 cnt = 2 if inside else 1
                 crow = (r + ring) * cols
-                h, c_new = cell(gss[ch], base + (r - r0) * cols, cnt * cols, cms[s][pl.ds(crow, cnt * cols), :])
+                c_old = cms[s][pl.ds(crow, cnt * cols), :]
+                h, c_new = cell(gss[ch], base + (r - r0) * cols, cnt * cols, c_old)
+                if skip is not None:
+                    c_new = jnp.where(skip, c_old, c_new)
                 cms[s][pl.ds(crow, cnt * cols), :] = c_new
                 if not inside:
                     h = h * (top_ok if r < 0 else bot_ok)
                 hb16 = h.astype(BF16)
                 if inside:
-                    ob[s, j, pl.ds(r * cols, cnt * cols), :] = hb16
+                    hout[t, s, pl.ds(r * cols, cnt * cols), :] = hb16
                 h = hb16.astype(F32)
                 for i in range(cnt):
-                    dst[pl.ds(h_addr(r + i, 0), cols), :] = h[i * cols:(i + 1) * cols]
+                    new = h[i * cols:(i + 1) * cols]
+                    if skip is not None:
+                        new = jnp.where(skip, dst[pl.ds(h_addr(r + i, 0), cols), :], new)
+                    dst[pl.ds(h_addr(r + i, 0), cols), :] = new
                 r += cnt
 
-        def out_copy(s, j, b):
-            return pltpu.make_async_copy(ob.at[s, j], hout.at[b * BLOCK + j, s], osem.at[s, j])
+        last = (BLOCK - 1, 2)
 
         def block(b, _):
             par = lax.rem(b, 2)
             for s in range(seqs):
-                wait_recv(s, par)
+                o = 1 - s
+                wait_all(rsem.at[par, s], msg_side, msg_corner)
                 if s == 0:
                     for j in range(BLOCK):
-                        for k in range(8):
-                            @pl.when(exists(k))
-                            def _():
-                                x_copy(b * BLOCK + j, opposite(k)).wait_recv()
-
-                @pl.when(b > 0)
-                def _():
-                    for j in range(BLOCK):
-                        out_copy(s, j, b - 1).wait()
-
+                        wait_all(xrsem.at[par, j], x_side, x_corner)
+                        wait_all(xssem.at[j], x_side, x_corner)
+                    wait_all(ssem.at[o], msg_side, msg_corner, b > 0)
+                else:
+                    wait_all(ssem.at[o], msg_side, msg_corner)
                 unpack(s, par)
+                build_xg(s, b * BLOCK, BLOCK - 1)
+                build_lhs(s, 0, 0)
+                if s == 0:
+                    elementwise(o, *last, lax.rem(b * BLOCK - 1 + steps, steps), b == 0)
+                    pack(o)
+                    send(o, par)
+                else:
+                    elementwise(o, *last, b * BLOCK + BLOCK - 1)
+                    pack(o)
+                    send(o, 1 - par, b < nblock - 1)
                 late = None
                 for j in range(BLOCK):
-                    build_xg(s, b * BLOCK + j, BLOCK - 1 - j)
+                    if j > 0:
+                        build_xg(s, b * BLOCK + j, BLOCK - 1 - j)
+                    if s == 0 and j == BLOCK - 1:
+                        for q in range(BLOCK):
+                            prep_x(lax.rem((b + 1) * BLOCK + q, steps))
+                        for q in range(BLOCK):
+                            send_x(lax.rem((b + 1) * BLOCK + q, steps), b < nblock - 1)
                     for ch in range(3):
-                        build_lhs(s, j, ch)
+                        if j + ch > 0:
+                            build_lhs(s, j, ch)
                         matmul(j, ch)
                         if late is not None:
-                            elementwise(s, *late)
+                            elementwise(s, *late, b * BLOCK + late[0])
                         late = (j, ch)
-                elementwise(s, *late)
-                wait_send(s)
-
-                @pl.when(b < nblock - 1)
-                def _():
-                    pack(s)
-                    send(s, 1 - par)
-
-                for j in range(BLOCK):
-                    out_copy(s, j, b).start()
             return 0
 
         lax.fori_loop(0, nblock, block, 0)
-
-        fin = [pltpu.make_async_copy(cms[s].at[pl.ds(ring * cols, rows * cols), :], cout.at[s], lsem.at[3 + s]) for s in range(seqs)]
-        for cp in fin:
-            cp.start()
-        for t in range(steps):
-            for k in range(8):
-                @pl.when(exists(k))
-                def _():
-                    x_copy(t, k).wait_send()
+        elementwise(1, *last, steps - 1)
+        wait_all(ssem.at[1], msg_side, msg_corner)
         for s in range(seqs):
-            for j in range(BLOCK):
-                out_copy(s, j, nblock - 1).wait()
-        for cp in fin:
-            cp.wait()
+            cout[s] = cms[s][pl.ds(ring * cols, rows * cols), :]
 
     hbuf = pltpu.VMEM((hrows * pitch, hid), F32)
     xbuf = pltpu.VMEM((hrows * pitch, 128), F32)
@@ -413,7 +425,8 @@
         + [pltpu.VMEM((mmax[ch], kdim), BF16) for ch in range(3)]
         + [pltpu.VMEM((mmax[ch], gates), F32) for ch in range(3)]
         + [
-            pltpu.VMEM((seqs, BLOCK, rows * cols, hid), BF16),
+            pltpu.VMEM((3, 3, chan, gates), BF16),
+            pltpu.VMEM((1, gates), F32),
             pltpu.VMEM((seqs, rows * cols, hid), BF16),
             pltpu.VMEM((seqs, 4, 80, hid), BF16),
             pltpu.VMEM((seqs, 4, ring * cols, hid), F32),
@@ -425,12 +438,11 @@
             pltpu.VMEM((2, seqs, 4, 8, hid), F32),
             pltpu.VMEM((16, hid), F32),
             pltpu.VMEM((2, 32, hid), F32),
-            pltpu.SemaphoreType.DMA((5,)),
-            pltpu.SemaphoreType.DMA((seqs, BLOCK)),
-            pltpu.SemaphoreType.DMA((seqs, 8, 2)),
-            pltpu.SemaphoreType.DMA((2, seqs, 8, 2)),
-            pltpu.SemaphoreType.DMA((steps, 8)),
-            pltpu.SemaphoreType.DMA((steps, 8)),
+            pltpu.SemaphoreType.DMA((8,)),
+            pltpu.SemaphoreType.DMA((seqs,)),
+            pltpu.SemaphoreType.DMA((2, seqs)),
+            pltpu.SemaphoreType.DMA((BLOCK,)),
+            pltpu.SemaphoreType.DMA((2, BLOCK)),
         ]
     )
     return kernel, scratch
@@ -447,22 +459,27 @@
         hid = h_init.shape[-1]
         gates = 4 * hid
         kernel, scratch = make_kernel(steps, seqs, rows, cols, chan, hid, row_count, col_count)
-        anyspace = pl.BlockSpec(memory_space=pl.ANY)
+        hbm = pl.BlockSpec(memory_space=pltpu.HBM)
         vmem = pl.BlockSpec(memory_space=pltpu.VMEM)
         ft = frames.transpose(0, 1, 2, 4, 3).reshape(steps * seqs, rows * chan, cols)
         all_hidden, cell_last = pl.pallas_call(
             kernel,
             out_shape=(
-                jax.ShapeDtypeStruct((steps, seqs, rows * cols, hid), BF16),
-                jax.ShapeDtypeStruct((seqs, rows * cols, hid), F32),
+                pltpu.VMEM((steps, seqs, rows * cols, hid), BF16),
+                pltpu.VMEM((seqs, rows * cols, hid), F32),
             ),
-            in_specs=[anyspace, vmem, anyspace, vmem, anyspace, anyspace],
-            out_specs=(anyspace, anyspace),
+            in_specs=[hbm] * 6,
+            out_specs=(vmem, vmem),
             scratch_shapes=scratch,
-            compiler_params=pltpu.CompilerParams(collective_id=0, has_side_effects=True, vmem_limit_bytes=60 * 1024 * 1024),
+            compiler_params=pltpu.CompilerParams(collective_id=0, has_side_effects=True, vmem_limit_bytes=44 * 1024 * 1024),
         )(
-            ft, w_x, w_h.reshape(9 * hid, gates), gate_bias.reshape(1, gates),
-            h_init.reshape(seqs, rows * cols, hid), c_init.reshape(seqs, rows * cols, hid),
+            *[
+                pltpu.with_memory_space_constraint(x, pltpu.HBM)
+                for x in (
+                    ft, w_x, w_h.reshape(9 * hid, gates), gate_bias.reshape(1, gates),
+                    h_init.reshape(seqs, rows * cols, hid), c_init.reshape(seqs, rows * cols, hid),
+                )
+            ]
         )
         return all_hidden.reshape(steps, seqs, rows, cols, hid), cell_last.reshape(seqs, rows, cols, hid)
 

time: 61.6 us -> 54.8 us (0.89)
  Pallas kernels: 55.5 us -> 51.5 us
  local copies, waits for them, and re-layouts: 5.31 us -> 2.61 us
    pallas_call x1, Pallas kernels: 55.5 us -> 51.5 us  [local_run(): pl.pallas_call(kernel, out_shape=(pltpu.VMEM((steps, seqs, rows * cols, h...]
    unnamed x4 -> x2, local copies, waits for them, and re-layouts: 5.31 us -> 2.61 us
where the time goes in v2:
time: 54.8 us
  Pallas kernels  51.5 us (94%)
  local copies, waits for them, and re-layouts  2.61 us (5%)
  between operations  0.64 us (1%)
    pallas_call x1, Pallas kernels, local_run(): pl.pallas_call(kernel, out_shape=(pltpu.VMEM((steps, seqs, rows * cols, h...  51.5 us
    unnamed x2, local copies, waits for them, and re-layouts  2.61 us

profile of v2, /device:TPU:97, one launch (start us, length us, event | category | flops | bytes accessed | tf_op | source)
XLA Modules:
  0.0 54.8 jit_solution(16552341136395855101)
XLA Ops:
  0.6 51.5 %shard_map.77 = (bf16[12,2,576,128]{3,2,1,0:T(8,128)(2,1)S(1)}, f32[2,576,128]{2,1,0:T(8,128)S(1)}) custom-call(bf16[24,384,24]{2,1,0:T(8,128)(2,1)} %bitcast.11, bf16[3,3,16,512]{3,2,1,0:T(8,128)(2,1)} %wx_hbm.1, bf16[1152,512]{1,0:T(8,128)(2,1)} %bitcast.12, f32[1,512]{1,0:T(1,128)} %bitcast.15, bf16[2,576,128]{2,1,0:T(8,128)(2,1)} %bitcast.14, ...), custom_call_target="tpu_custom_call" | custom-call | tf_op jit(solution)/shard_map/pallas_call | solution.py:465
  52.2 1.8 %copy.10 = bf16[12,2,24,24,128]{4,3,2,1,0:T(8,128)(2,1)} copy(bf16[12,2,24,24,128]{4,3,2,1,0:T(8,128)(2,1)S(1)} %bitcast.9) | data formatting | bytes 7077888
  54.0 0.8 %copy.11 = f32[2,24,24,128]{3,2,1,0:T(8,128)} copy(f32[2,24,24,128]{3,2,1,0:T(8,128)S(1)} %bitcast.10) | data formatting | bytes 1179648

commit v3 on v2

--- a/solution.py
+++ b/solution.py
@@ -39,7 +39,7 @@
 
     def kernel(frames, wx_hbm, wh_hbm, bias_hbm, hinit, cinit, hout, cout, *scratch):
         (hb0a, hb1a, hb2a, hb0b, hb1b, hb2b, xga, xgb, cma, cmb, csa, csb, xt, fbuf, wall,
-         lhs0, lhs1, lhs2, gs0, gs1, gs2, wx_ref, bias_ref, hin, sh, sc, sch, scc, rh, rc, rch, rcc, tmp, smask,
+         lhs0, lhs1, lhs2, gs0, gs1, gs2, wx_ref, bias_ref, hin, sh, sc, sq, rh, rc, rq, smask,
          lsem, ssem, rsem, xssem, xrsem) = scratch
         hbs = ((hb0a, hb1a, hb2a), (hb0b, hb1b, hb2b))
         xgs = (xga, xgb)
@@ -68,7 +68,17 @@
             return out
 
         def dev(k):
-            return {"rows": ri + DIRS[k][0], "cols": ci + DIRS[k][1]}
+            return {
+                "rows": lax.rem(ri + DIRS[k][0] + row_count, row_count),
+                "cols": lax.rem(ci + DIRS[k][1] + col_count, col_count),
+            }
+
+        present = [exists(k) for k in range(8)]
+        n_row = jnp.where(ri > 0, 1, 0) + jnp.where(ri < row_count - 1, 1, 0)
+        n_col = jnp.where(ci > 0, 1, 0) + jnp.where(ci < col_count - 1, 1, 0)
+
+        def pick(k, dst, real, spare):
+            return jnp.where(jnp.logical_and(present[k], dst < nblock), real, spare)
 
         def h_addr(r, c):
             return (r + BLOCK) * pitch + COL0 + c
@@ -94,10 +104,8 @@
         cp_g.start()
 
         barrier = pltpu.get_barrier_semaphore()
-        rh[...] = jnp.zeros_like(rh)
-        rc[...] = jnp.zeros_like(rc)
-        rch[...] = jnp.zeros_like(rch)
-        rcc[...] = jnp.zeros_like(rcc)
+        for ref in (rh, rc, rq):
+            ref[pl.ds(0, 2)] = jnp.zeros((2,) + ref.shape[1:], ref.dtype)
 
         xlanes = xt.shape[2]
 
@@ -110,9 +118,7 @@
 
         lax.fori_loop(0, steps * seqs, zero_x, 0)
         for k in range(8):
-            @pl.when(exists(k))
-            def _():
-                pl.semaphore_signal(barrier, 1, device_id=dev(k), device_id_type=MESH)
+            pl.semaphore_signal(barrier, 1, device_id=dev(k), device_id_type=MESH)
         top_ok = jnp.where(ri > 0, 1.0, 0.0).astype(F32)
         bot_ok = jnp.where(ri < row_count - 1, 1.0, 0.0).astype(F32)
         left_ok = jnp.where(ci > 0, 1.0, 0.0).astype(F32)
@@ -122,18 +128,18 @@
         smask[0] = rmask * left_ok
         smask[1] = rmask * right_ok
 
-        n_row = jnp.where(ri > 0, 1, 0) + jnp.where(ri < row_count - 1, 1, 0)
-        n_col = jnp.where(ci > 0, 1, 0) + jnp.where(ci < col_count - 1, 1, 0)
-        pl.semaphore_wait(barrier, (n_row + 1) * (n_col + 1) - 1)
-
-        def msg_copies(s, k, par):
+        pl.semaphore_wait(barrier, 8)
+
+        def msg_copies(s, k, dst):
+            slot = pick(k, dst, lax.rem(dst, 2), 2 + dst)
+            sem = pick(k, dst, lax.rem(dst, 2) * seqs + s, 2 * seqs + dst * seqs + s)
             if k < 4:
-                pairs = ((sh.at[s, k], rh.at[par, s, k]), (sc.at[s, k], rc.at[par, s, k]))
+                pairs = ((sh.at[s, k], rh.at[slot, s, k]), (sc.at[s, k], rc.at[slot, s, k]))
             else:
-                pairs = ((sch.at[s, k - 4], rch.at[par, s, k - 4]), (scc.at[s, k - 4], rcc.at[par, s, k - 4]))
+                pairs = ((sq.at[s, k - 4], rq.at[slot, s, k - 4]),)
             return [
-                pltpu.make_async_remote_copy(src_ref=a, dst_ref=b, send_sem=ssem.at[s], recv_sem=rsem.at[par, s], device_id=dev(k), device_id_type=MESH)
-                for n, (a, b) in enumerate(pairs)
+                pltpu.make_async_remote_copy(src_ref=a, dst_ref=b, send_sem=ssem.at[s], recv_sem=rsem.at[sem], device_id=dev(k), device_id_type=MESH)
+                for a, b in pairs
             ]
 
         def pack(s):
@@ -156,10 +162,9 @@
                         sc[s, k, pl.ds(j * rows, rows), :] = cm[pl.ds(ring * cols + cc0 + j, rows, stride=cols), :]
                 else:
                     for i in range(BLOCK):
-                        tmp[pl.ds(i * BLOCK, BLOCK), :] = hb[pl.ds(h_addr(r0 + i, c0), BLOCK), :]
-                    sch[s, k - 4] = tmp[pl.ds(0, 16), :].astype(BF16)
+                        sq[s, k - 4, pl.ds(i * BLOCK, BLOCK), :] = hb[pl.ds(h_addr(r0 + i, c0), BLOCK), :]
                     for j in range(ring):
-                        scc[s, k - 4, pl.ds(j * ring, ring), :] = cm[pl.ds((rc0 + ring) * cols + cc0 + j, ring, stride=cols), :]
+                        sq[s, k - 4, pl.ds(BLOCK * BLOCK + j * ring, ring), :] = cm[pl.ds((rc0 + ring) * cols + cc0 + j, ring, stride=cols), :]
 
         def unpack(s, par):
             hb = hbs[s][0]
@@ -184,36 +189,39 @@
                     for j in range(ring):
                         cs[pl.ds((st0 + j) * 32 + ring, rows), :] = rc[par, s, o, pl.ds(j * rows, rows), :]
                 else:
-                    tmp[pl.ds(0, 16), :] = rch[par, s, o - 4].astype(F32)
                     for i in range(BLOCK):
-                        hb[pl.ds(h_addr(r0 + i, c0), BLOCK), :] = tmp[pl.ds(i * BLOCK, BLOCK), :]
+                        hb[pl.ds(h_addr(r0 + i, c0), BLOCK), :] = rq[par, s, o - 4, pl.ds(i * BLOCK, BLOCK), :]
                     for j in range(ring):
-                        cs[pl.ds((st0 + j) * 32 + q0, ring), :] = rcc[par, s, o - 4, pl.ds(j * ring, ring), :]
-
-        def send(s, par, more=None):
+                        cs[pl.ds((st0 + j) * 32 + q0, ring), :] = rq[par, s, o - 4, pl.ds(BLOCK * BLOCK + j * ring, ring), :]
+
+        def send(s, dst):
             for k in range(8):
-                @pl.when(exists(k) if more is None else jnp.logical_and(exists(k), more))
-                def _():
-                    for cp in msg_copies(s, k, par):
-                        cp.start()
-
-        def wait_all(sem, side, corner, more=None):
+                for cp in msg_copies(s, k, dst):
+                    cp.start()
+
+        def wait_rows(sem, n):
+            pltpu.make_async_copy(cinit.at[:, pl.ds(0, n // seqs)], cout.at[:, pl.ds(0, n // seqs)], sem).wait()
+
+        def wait_all(sem, side, corner, absent=False):
             for a in ((1, 2) if row_count > 2 else (row_count - 1,)):
                 for b in ((1, 2) if col_count > 2 else (col_count - 1,)):
                     n = side * (a + b) + corner * a * b
-                    cond = jnp.logical_and(n_row == a, n_col == b)
-
-                    @pl.when(cond if more is None else jnp.logical_and(cond, more))
-                    def _():
-                        pltpu.make_async_copy(cinit.at[0, pl.ds(0, n)], cma.at[pl.ds(0, n)], sem).wait()
+                    if absent:
+                        n = 4 * side + 4 * corner - n
+                    if n:
+                        @pl.when(jnp.logical_and(n_row == a, n_col == b))
+                        def _():
+                            wait_rows(sem, n)
 
         msg_side, msg_corner = 40 + ring * cols, 16
-        x_side, x_corner = seqs * cols, seqs * 8
+        x_side, x_corner = BLOCK * seqs * cols, BLOCK * seqs * 8
+        msg_total = 4 * (msg_side + msg_corner)
+        x_total = 4 * (x_side + x_corner)
 
         own_lane = xrow0 * chan
         row_lanes = rows * chan
 
-        def x_copy(t, k):
+        def x_copy(dst, k):
             dr, dc = DIRS[k]
             if dr == 0:
                 lanes_s, lanes_d, lane_n = own_lane, own_lane, row_lanes
@@ -227,10 +235,40 @@
                 sub_n = 8
                 sub_s = COL0 if dc < 0 else COL0 + cols - 8
                 sub_d = COL0 + cols if dc < 0 else 0
+            return make_x_copy(dst, k, sub_s, sub_d, sub_n, lanes_s, lanes_d, lane_n, xssem.at[0], 0, 0)
+
+        def make_x_copy(dst, k, sub_s, sub_d, sub_n, lanes_s, lanes_d, lane_n, ssem_x, real, spare):
+            per = BLOCK * seqs
             return pltpu.make_async_remote_copy(
-                src_ref=xt.at[pl.ds(t * seqs, seqs), pl.ds(sub_s, sub_n), pl.ds(lanes_s, lane_n)],
-                dst_ref=xt.at[pl.ds(t * seqs, seqs), pl.ds(sub_d, sub_n), pl.ds(lanes_d, lane_n)],
-                send_sem=xssem.at[lax.rem(t, BLOCK)], recv_sem=xrsem.at[lax.rem(lax.div(t, BLOCK), 2), lax.rem(t, BLOCK)], device_id=dev(k), device_id_type=MESH)
+                src_ref=xt.at[pl.ds(lax.rem(dst, nblock) * per, per), pl.ds(sub_s, sub_n), pl.ds(lanes_s, lane_n)],
+                dst_ref=xt.at[pl.ds(pick(k, dst, dst, nblock + dst) * per, per), pl.ds(sub_d, sub_n), pl.ds(lanes_d, lane_n)],
+                send_sem=ssem_x, recv_sem=xrsem.at[pick(k, dst, real, XSPARE + spare)], device_id=dev(k), device_id_type=MESH)
+
+        XSPARE = 5
+
+        def x_rows(dst, k):
+            up = k == 0
+            return make_x_copy(
+                dst, k, COL0, COL0, cols, own_lane if up else own_lane + row_lanes - 128, own_lane + row_lanes if up else 0, 128,
+                xssem.at[1], 1 + lax.rem(dst, 2), 1 + dst)
+
+        def x_cols(dst, k):
+            left = k == 2
+            return make_x_copy(
+                dst, k, COL0 if left else COL0 + cols - 8, COL0 + cols if left else 0, 8, 0, 0, xlanes,
+                xssem.at[2], 3 + lax.rem(dst, 2), 2 + nblock + dst)
+
+        def wait_axis(sem, count, size, more=None, absent=False):
+            for a in (0, 1, 2):
+                n = (2 - a if absent else a) * size
+                cond = count == a
+                if n:
+                    @pl.when(cond if more is None else jnp.logical_and(cond, more))
+                    def _():
+                        wait_rows(sem, n)
+
+        xr_size = BLOCK * seqs * cols
+        xc_size = BLOCK * seqs * 8 * (xlanes // 128)
 
         def load_state(s):
             for r in range(0, rows, 2):
@@ -246,26 +284,20 @@
 
         eye = (lax.broadcasted_iota(jnp.int32, (cols, cols), 0) == lax.broadcasted_iota(jnp.int32, (cols, cols), 1)).astype(F32).astype(BF16)
 
-        def prep_x(t):
-            for s in range(seqs):
-                xt[t * seqs + s, pl.ds(COL0, cols), pl.ds(own_lane, row_lanes)] = lax.dot_general(
-                    eye, fbuf[t * seqs + s], (((1,), (1,)), ((), ())), preferred_element_type=F32)
-
-        def send_x(t, more=None):
-            for k in range(8):
-                @pl.when(exists(k) if more is None else jnp.logical_and(exists(k), more))
-                def _():
-                    x_copy(t, k).start()
+        def prep_x(dst):
+            for q in range(BLOCK):
+                t = dst * BLOCK + q
+                for s in range(seqs):
+                    xt[t * seqs + s, pl.ds(COL0, cols), pl.ds(own_lane, row_lanes)] = lax.dot_general(
+                        eye, fbuf[lax.rem(t, steps) * seqs + s], (((1,), (1,)), ((), ())), preferred_element_type=F32)
+
 
         cp_f.wait()
-        for t in range(BLOCK):
-            prep_x(t)
-        for t in range(BLOCK):
-            send_x(t)
+        prep_x(0)
+        for k in range(8):
+            x_copy(0, k).start()
         load_state(1)
         cp_c[1].wait()
-        cp_g.wait()
-
         cp_w.wait()
         for cp in cp_small:
             cp.wait()
@@ -274,6 +306,14 @@
             for dr in range(3):
                 wall[pl.ds(9 * hid + dc * 128 + dr * chan, chan), :] = wx_ref[dr, dc]
 
+        cp_g.wait()
+
+        def prep_more(dst, _):
+            prep_x(dst)
+            return 0
+
+        lax.fori_loop(1, nblock, prep_more, 0)
+        wait_all(xrsem.at[0], x_side, x_corner)
         lane = lax.broadcasted_iota(jnp.int32, (pitch, 128), 1)
 
         def build_xg(s, t, ext):
@@ -367,34 +407,37 @@
             par = lax.rem(b, 2)
             for s in range(seqs):
                 o = 1 - s
-                wait_all(rsem.at[par, s], msg_side, msg_corner)
+                wait_all(rsem.at[par * seqs + s], msg_side, msg_corner)
                 if s == 0:
-                    for j in range(BLOCK):
-                        wait_all(xrsem.at[par, j], x_side, x_corner)
-                        wait_all(xssem.at[j], x_side, x_corner)
-                    wait_all(ssem.at[o], msg_side, msg_corner, b > 0)
+                    @pl.when(b > 0)
+                    def _():
+                        wait_rows(ssem.at[o], msg_total)
+                        wait_rows(xssem.at[2], 2 * xc_size)
+
+                    wait_axis(xrsem.at[3 + par], n_col, xc_size, b > 0)
                 else:
-                    wait_all(ssem.at[o], msg_side, msg_corner)
+                    wait_rows(ssem.at[o], msg_total)
+                    wait_rows(xssem.at[1], 2 * xr_size)
+                    wait_axis(xrsem.at[1 + lax.rem(b + 1, 2)], n_row, xr_size, b < nblock - 1)
                 unpack(s, par)
                 build_xg(s, b * BLOCK, BLOCK - 1)
                 build_lhs(s, 0, 0)
                 if s == 0:
                     elementwise(o, *last, lax.rem(b * BLOCK - 1 + steps, steps), b == 0)
                     pack(o)
-                    send(o, par)
+                    send(o, b)
+                    for k in (0, 1):
+                        x_rows(b + 1, k).start()
                 else:
                     elementwise(o, *last, b * BLOCK + BLOCK - 1)
                     pack(o)
-                    send(o, 1 - par, b < nblock - 1)
+                    send(o, b + 1)
+                    for k in (2, 3):
+                        x_cols(b + 1, k).start()
                 late = None
                 for j in range(BLOCK):
                     if j > 0:
                         build_xg(s, b * BLOCK + j, BLOCK - 1 - j)
-                    if s == 0 and j == BLOCK - 1:
-                        for q in range(BLOCK):
-                            prep_x(lax.rem((b + 1) * BLOCK + q, steps))
-                        for q in range(BLOCK):
-                            send_x(lax.rem((b + 1) * BLOCK + q, steps), b < nblock - 1)
                     for ch in range(3):
                         if j + ch > 0:
                             build_lhs(s, j, ch)
@@ -406,7 +449,20 @@
 
         lax.fori_loop(0, nblock, block, 0)
         elementwise(1, *last, steps - 1)
-        wait_all(ssem.at[1], msg_side, msg_corner)
+        wait_rows(ssem.at[0], msg_total)
+        wait_rows(ssem.at[1], msg_total)
+        wait_rows(xssem.at[0], x_total)
+        wait_rows(xssem.at[2], 2 * xc_size)
+        for dst in range(nblock):
+            for s in range(seqs):
+                wait_all(rsem.at[(2 + dst) * seqs + s], msg_side, msg_corner, absent=True)
+        wait_all(xrsem.at[XSPARE], x_side, x_corner, absent=True)
+        for dst in range(1, nblock):
+            wait_axis(xrsem.at[XSPARE + 1 + dst], n_row, xr_size, absent=True)
+            wait_axis(xrsem.at[XSPARE + 2 + nblock + dst], n_col, xc_size, absent=True)
+        wait_rows(rsem.at[(2 + nblock) * seqs], msg_total)
+        wait_rows(xrsem.at[XSPARE + 1 + nblock], 2 * xr_size)
+        wait_rows(xrsem.at[XSPARE + 2 + 2 * nblock], 2 * xc_size)
         for s in range(seqs):
             cout[s] = cms[s][pl.ds(ring * cols, rows * cols), :]
 
@@ -418,7 +474,7 @@
         + [pltpu.VMEM(((rows + 2 * ring) * cols, hid), F32)] * 2
         + [pltpu.VMEM((nstrip * 32, hid), F32)] * 2
         + [
-            pltpu.VMEM((steps * seqs, pitch, (rows + 16) * chan), F32),
+            pltpu.VMEM(((2 * nblock + 1) * BLOCK * seqs, pitch, (rows + 16) * chan), F32),
             pltpu.VMEM((steps * seqs, rows * chan, cols), BF16),
             pltpu.VMEM((kdim, gates), BF16),
         ]
@@ -430,19 +486,16 @@
             pltpu.VMEM((seqs, rows * cols, hid), BF16),
             pltpu.VMEM((seqs, 4, 80, hid), BF16),
             pltpu.VMEM((seqs, 4, ring * cols, hid), F32),
-            pltpu.VMEM((seqs, 4, 16, hid), BF16),
-            pltpu.VMEM((seqs, 4, 8, hid), F32),
-            pltpu.VMEM((2, seqs, 4, 80, hid), BF16),
-            pltpu.VMEM((2, seqs, 4, ring * cols, hid), F32),
-            pltpu.VMEM((2, seqs, 4, 16, hid), BF16),
-            pltpu.VMEM((2, seqs, 4, 8, hid), F32),
-            pltpu.VMEM((16, hid), F32),
+            pltpu.VMEM((seqs, 4, 16, hid), F32),
+            pltpu.VMEM((3 + nblock, seqs, 4, 80, hid), BF16),
+            pltpu.VMEM((3 + nblock, seqs, 4, ring * cols, hid), F32),
+            pltpu.VMEM((3 + nblock, seqs, 4, 16, hid), F32),
             pltpu.VMEM((2, 32, hid), F32),
             pltpu.SemaphoreType.DMA((8,)),
             pltpu.SemaphoreType.DMA((seqs,)),
-            pltpu.SemaphoreType.DMA((2, seqs)),
-            pltpu.SemaphoreType.DMA((BLOCK,)),
-            pltpu.SemaphoreType.DMA((2, BLOCK)),
+            pltpu.SemaphoreType.DMA(((3 + nblock) * seqs,)),
+            pltpu.SemaphoreType.DMA((3,)),
+            pltpu.SemaphoreType.DMA((8 + 2 * nblock,)),
         ]
     )
     return kernel, scratch

time: 54.8 us -> 59.2 us (1.080)
  Pallas kernels: 51.5 us -> 55.9 us
    pallas_call x1, Pallas kernels: 51.5 us -> 55.9 us  [local_run(): pl.pallas_call(kernel, out_shape=(pltpu.VMEM((steps, seqs, rows * cols, h...]
where the time goes in v3:
time: 59.2 us; the launch traced here: 59.1 us
  Pallas kernels  55.9 us (94%)
  local copies, waits for them, and re-layouts  2.61 us (4%)
  between operations  0.64 us (1%)
    pallas_call x1, Pallas kernels, local_run(): pl.pallas_call(kernel, out_shape=(pltpu.VMEM((steps, seqs, rows * cols, h...  55.9 us
    unnamed x2, local copies, waits for them, and re-layouts  2.61 us

profile of v3, /device:TPU:97, one launch (start us, length us, event | category | flops | bytes accessed | tf_op | source)
XLA Modules:
  0.0 59.1 jit_solution(13995342246611945486)
XLA Ops:
  0.6 55.9 %shard_map.77 = (bf16[12,2,576,128]{3,2,1,0:T(8,128)(2,1)S(1)}, f32[2,576,128]{2,1,0:T(8,128)S(1)}) custom-call(bf16[24,384,24]{2,1,0:T(8,128)(2,1)} %bitcast.11, bf16[3,3,16,512]{3,2,1,0:T(8,128)(2,1)} %wx_hbm.1, bf16[1152,512]{1,0:T(8,128)(2,1)} %bitcast.12, f32[1,512]{1,0:T(1,128)} %bitcast.15, bf16[2,576,128]{2,1,0:T(8,128)(2,1)} %bitcast.14, ...), custom_call_target="tpu_custom_call" | custom-call | tf_op jit(solution)/shard_map/pallas_call | solution.py:518
  56.5 1.8 %copy.10 = bf16[12,2,24,24,128]{4,3,2,1,0:T(8,128)(2,1)} copy(bf16[12,2,24,24,128]{4,3,2,1,0:T(8,128)(2,1)S(1)} %bitcast.9) | data formatting | bytes 7077888
  58.3 0.8 %copy.11 = f32[2,24,24,128]{3,2,1,0:T(8,128)} copy(f32[2,24,24,128]{3,2,1,0:T(8,128)S(1)} %bitcast.10) | data formatting | bytes 1179648

commit v4 on v3

--- a/solution.py
+++ b/solution.py
@@ -39,7 +39,7 @@
 
     def kernel(frames, wx_hbm, wh_hbm, bias_hbm, hinit, cinit, hout, cout, *scratch):
         (hb0a, hb1a, hb2a, hb0b, hb1b, hb2b, xga, xgb, cma, cmb, csa, csb, xt, fbuf, wall,
-         lhs0, lhs1, lhs2, gs0, gs1, gs2, wx_ref, bias_ref, hin, sh, sc, sq, rh, rc, rq, smask,
+         lhs0, lhs1, lhs2, gs0, gs1, gs2, wx_ref, bias_ref, hin, sh, sc, sq, rh, rc, rq, xs, xr, xtmp, xtmp2, smask,
          lsem, ssem, rsem, xssem, xrsem) = scratch
         hbs = ((hb0a, hb1a, hb2a), (hb0b, hb1b, hb2b))
         xgs = (xga, xgb)
@@ -67,15 +67,16 @@
                 out = jnp.logical_and(out, extra)
             return out
 
-        def dev(k):
-            return {
-                "rows": lax.rem(ri + DIRS[k][0] + row_count, row_count),
-                "cols": lax.rem(ci + DIRS[k][1] + col_count, col_count),
-            }
+        def dev(k, dst=0):
+            real = jnp.logical_and(present[k], dst < nblock)
+            return {"rows": jnp.where(real, ri + DIRS[k][0], partner), "cols": jnp.where(real, ci + DIRS[k][1], ci)}
 
         present = [exists(k) for k in range(8)]
+        partner = jnp.where(lax.rem(ri, 2) == 0, ri + 1, ri - 1)
         n_row = jnp.where(ri > 0, 1, 0) + jnp.where(ri < row_count - 1, 1, 0)
         n_col = jnp.where(ci > 0, 1, 0) + jnp.where(ci < col_count - 1, 1, 0)
+
+        p_row = jnp.where(partner > 0, 1, 0) + jnp.where(partner < row_count - 1, 1, 0)
 
         def pick(k, dst, real, spare):
             return jnp.where(jnp.logical_and(present[k], dst < nblock), real, spare)
@@ -106,12 +107,11 @@
         barrier = pltpu.get_barrier_semaphore()
         for ref in (rh, rc, rq):
             ref[pl.ds(0, 2)] = jnp.zeros((2,) + ref.shape[1:], ref.dtype)
+        xr[...] = jnp.zeros_like(xr)
 
         xlanes = xt.shape[2]
 
         def zero_x(i, _):
-            for sub in (0, COL0 + cols):
-                xt[i, pl.ds(sub, 8), :] = jnp.zeros((8, xlanes), F32)
             for lane0 in (0, xlanes - 128):
                 xt[i, pl.ds(COL0, cols), pl.ds(lane0, 128)] = jnp.zeros((cols, 128), F32)
             return 0
@@ -128,7 +128,8 @@
         smask[0] = rmask * left_ok
         smask[1] = rmask * right_ok
 
-        pl.semaphore_wait(barrier, 8)
+        met = (n_row + 1) * (n_col + 1) - 1
+        pl.semaphore_wait(barrier, met + 8 - ((p_row + 1) * (n_col + 1) - 1))
 
         def msg_copies(s, k, dst):
             slot = pick(k, dst, lax.rem(dst, 2), 2 + dst)
@@ -138,7 +139,7 @@
             else:
                 pairs = ((sq.at[s, k - 4], rq.at[slot, s, k - 4]),)
             return [
-                pltpu.make_async_remote_copy(src_ref=a, dst_ref=b, send_sem=ssem.at[s], recv_sem=rsem.at[sem], device_id=dev(k), device_id_type=MESH)
+                pltpu.make_async_remote_copy(src_ref=a, dst_ref=b, send_sem=ssem.at[s], recv_sem=rsem.at[sem], device_id=dev(k, dst), device_id_type=MESH)
                 for a, b in pairs
             ]
 
@@ -202,73 +203,65 @@
         def wait_rows(sem, n):
             pltpu.make_async_copy(cinit.at[:, pl.ds(0, n // seqs)], cout.at[:, pl.ds(0, n // seqs)], sem).wait()
 
-        def wait_all(sem, side, corner, absent=False):
+        def wait_all(sem, row_size, col_size, corner_size, absent=False, more=None):
             for a in ((1, 2) if row_count > 2 else (row_count - 1,)):
                 for b in ((1, 2) if col_count > 2 else (col_count - 1,)):
-                    n = side * (a + b) + corner * a * b
+                    n = row_size * a + col_size * b + corner_size * a * b
                     if absent:
-                        n = 4 * side + 4 * corner - n
+                        n = 2 * row_size + 2 * col_size + 4 * corner_size - n
+                    cond = jnp.logical_and((p_row if absent else n_row) == a, n_col == b)
                     if n:
-                        @pl.when(jnp.logical_and(n_row == a, n_col == b))
+                        @pl.when(cond if more is None else jnp.logical_and(cond, more))
                         def _():
                             wait_rows(sem, n)
 
         msg_side, msg_corner = 40 + ring * cols, 16
-        x_side, x_corner = BLOCK * seqs * cols, BLOCK * seqs * 8
         msg_total = 4 * (msg_side + msg_corner)
-        x_total = 4 * (x_side + x_corner)
 
         own_lane = xrow0 * chan
         row_lanes = rows * chan
 
-        def x_copy(dst, k):
+        def x_copy(first, count, k, sem):
             dr, dc = DIRS[k]
-            if dr == 0:
-                lanes_s, lanes_d, lane_n = own_lane, own_lane, row_lanes
+            if dc == 0:
+                per = BLOCK * seqs
+                src = own_lane if dr < 0 else own_lane + row_lanes - 128
+                dst = own_lane + row_lanes if dr < 0 else 0
+                a = xt.at[pl.ds(first * per, count * per), pl.ds(COL0, cols), pl.ds(src, 128)]
+                b = xt.at[pl.ds(first * per, count * per), pl.ds(COL0, cols), pl.ds(dst, 128)]
             else:
-                lane_n = 8 * chan
-                lanes_s = own_lane if dr < 0 else own_lane + row_lanes - lane_n
-                lanes_d = own_lane + row_lanes if dr < 0 else 0
-            if dc == 0:
-                sub_s, sub_d, sub_n = COL0, COL0, cols
-            else:
-                sub_n = 8
-                sub_s = COL0 if dc < 0 else COL0 + cols - 8
-                sub_d = COL0 + cols if dc < 0 else 0
-            return make_x_copy(dst, k, sub_s, sub_d, sub_n, lanes_s, lanes_d, lane_n, xssem.at[0], 0, 0)
-
-        def make_x_copy(dst, k, sub_s, sub_d, sub_n, lanes_s, lanes_d, lane_n, ssem_x, real, spare):
-            per = BLOCK * seqs
+                width = row_lanes if dr == 0 else 128
+                src = row_lanes - 128 if dr > 0 else 0
+                dst = {-1: own_lane + row_lanes, 0: own_lane, 1: 0}[dr]
+                a = xs.at[pl.ds(first, count), 0 if dc < 0 else 1, :, pl.ds(src, width)]
+                b = xr.at[pl.ds(first, count), 1 if dc < 0 else 0, :, pl.ds(dst, width)]
             return pltpu.make_async_remote_copy(
-                src_ref=xt.at[pl.ds(lax.rem(dst, nblock) * per, per), pl.ds(sub_s, sub_n), pl.ds(lanes_s, lane_n)],
-                dst_ref=xt.at[pl.ds(pick(k, dst, dst, nblock + dst) * per, per), pl.ds(sub_d, sub_n), pl.ds(lanes_d, lane_n)],
-                send_sem=ssem_x, recv_sem=xrsem.at[pick(k, dst, real, XSPARE + spare)], device_id=dev(k), device_id_type=MESH)
-
-        XSPARE = 5
-
-        def x_rows(dst, k):
-            up = k == 0
-            return make_x_copy(
-                dst, k, COL0, COL0, cols, own_lane if up else own_lane + row_lanes - 128, own_lane + row_lanes if up else 0, 128,
-                xssem.at[1], 1 + lax.rem(dst, 2), 1 + dst)
-
-        def x_cols(dst, k):
-            left = k == 2
-            return make_x_copy(
-                dst, k, COL0 if left else COL0 + cols - 8, COL0 + cols if left else 0, 8, 0, 0, xlanes,
-                xssem.at[2], 3 + lax.rem(dst, 2), 2 + nblock + dst)
-
-        def wait_axis(sem, count, size, more=None, absent=False):
-            for a in (0, 1, 2):
-                n = (2 - a if absent else a) * size
-                cond = count == a
-                if n:
-                    @pl.when(cond if more is None else jnp.logical_and(cond, more))
-                    def _():
-                        wait_rows(sem, n)
-
-        xr_size = BLOCK * seqs * cols
-        xc_size = BLOCK * seqs * 8 * (xlanes // 128)
+                src_ref=a, dst_ref=b, send_sem=xssem.at[sem], recv_sem=xrsem.at[sem], device_id=dev(k), device_id_type=MESH)
+
+        x_sizes = (BLOCK * seqs * cols, 16 * row_lanes // 256, 16 * 128 // 256)
+
+        def x_rows_of(s, q):
+            w = BLOCK - q
+            return s * (BLOCK * (BLOCK + 1) // 2) + sum(BLOCK - p for p in range(q)), w
+
+        def pack_x(blk):
+            for side in range(2):
+                for s in range(seqs):
+                    for q in range(BLOCK):
+                        at, w = x_rows_of(s, q)
+                        col = COL0 if side == 0 else COL0 + cols - w
+                        xtmp[side, pl.ds(at, w), :] = xt[(blk * BLOCK + q) * seqs + s, pl.ds(col, w), pl.ds(own_lane, row_lanes)]
+                xs[blk, side] = xtmp[side].astype(BF16)
+
+        def unpack_x(blk):
+            for side in range(2):
+                v = xr[blk, side].astype(F32)
+                xtmp2[side] = v
+                for s in range(seqs):
+                    for q in range(BLOCK):
+                        at, w = x_rows_of(s, q)
+                        col = COL0 - w if side == 0 else COL0 + cols
+                        xt[(blk * BLOCK + q) * seqs + s, pl.ds(col, w), :] = xtmp2[side, pl.ds(at, w), :]
 
         def load_state(s):
             for r in range(0, rows, 2):
@@ -289,13 +282,20 @@
                 t = dst * BLOCK + q
                 for s in range(seqs):
                     xt[t * seqs + s, pl.ds(COL0, cols), pl.ds(own_lane, row_lanes)] = lax.dot_general(
-                        eye, fbuf[lax.rem(t, steps) * seqs + s], (((1,), (1,)), ((), ())), preferred_element_type=F32)
+                        eye, fbuf[t * seqs + s], (((1,), (1,)), ((), ())), preferred_element_type=F32)
 
 
         cp_f.wait()
         prep_x(0)
-        for k in range(8):
-            x_copy(0, k).start()
+        pack_x(0)
+
+        def send_x(first, count, sem):
+            for k in range(8):
+                @pl.when(present[k])
+                def _():
+                    x_copy(first, count, k, sem).start()
+
+        send_x(0, 1, 0)
         load_state(1)
         cp_c[1].wait()
         cp_w.wait()
@@ -308,12 +308,15 @@
 
         cp_g.wait()
 
-        def prep_more(dst, _):
-            prep_x(dst)
+        def prep_more(blk, _):
+            prep_x(blk)
+            pack_x(blk)
             return 0
 
         lax.fori_loop(1, nblock, prep_more, 0)
-        wait_all(xrsem.at[0], x_side, x_corner)
+        send_x(1, nblock - 1, 1)
+        wait_all(xrsem.at[0], *x_sizes)
+        unpack_x(0)
         lane = lax.broadcasted_iota(jnp.int32, (pitch, 128), 1)
 
         def build_xg(s, t, ext):
@@ -407,18 +410,14 @@
             par = lax.rem(b, 2)
             for s in range(seqs):
                 o = 1 - s
-                wait_all(rsem.at[par * seqs + s], msg_side, msg_corner)
+                wait_all(rsem.at[par * seqs + s], msg_side, msg_side, msg_corner)
                 if s == 0:
                     @pl.when(b > 0)
                     def _():
                         wait_rows(ssem.at[o], msg_total)
-                        wait_rows(xssem.at[2], 2 * xc_size)
-
-                    wait_axis(xrsem.at[3 + par], n_col, xc_size, b > 0)
                 else:
                     wait_rows(ssem.at[o], msg_total)
-                    wait_rows(xssem.at[1], 2 * xr_size)
-                    wait_axis(xrsem.at[1 + lax.rem(b + 1, 2)], n_row, xr_size, b < nblock - 1)
+                    wait_all(xrsem.at[1], *[(nblock - 1) * n for n in x_sizes], more=b == 0)
                 unpack(s, par)
                 build_xg(s, b * BLOCK, BLOCK - 1)
                 build_lhs(s, 0, 0)
@@ -426,18 +425,16 @@
                     elementwise(o, *last, lax.rem(b * BLOCK - 1 + steps, steps), b == 0)
                     pack(o)
                     send(o, b)
-                    for k in (0, 1):
-                        x_rows(b + 1, k).start()
                 else:
                     elementwise(o, *last, b * BLOCK + BLOCK - 1)
                     pack(o)
                     send(o, b + 1)
-                    for k in (2, 3):
-                        x_cols(b + 1, k).start()
                 late = None
                 for j in range(BLOCK):
                     if j > 0:
                         build_xg(s, b * BLOCK + j, BLOCK - 1 - j)
+                    if s == seqs - 1 and j == BLOCK - 1:
+                        unpack_x(lax.rem(b + 1, nblock))
                     for ch in range(3):
                         if j + ch > 0:
                             build_lhs(s, j, ch)
@@ -451,18 +448,12 @@
         elementwise(1, *last, steps - 1)
         wait_rows(ssem.at[0], msg_total)
         wait_rows(ssem.at[1], msg_total)
-        wait_rows(xssem.at[0], x_total)
-        wait_rows(xssem.at[2], 2 * xc_size)
+        wait_all(xssem.at[0], *x_sizes)
+        wait_all(xssem.at[1], *[(nblock - 1) * n for n in x_sizes])
         for dst in range(nblock):
             for s in range(seqs):
-                wait_all(rsem.at[(2 + dst) * seqs + s], msg_side, msg_corner, absent=True)
-        wait_all(xrsem.at[XSPARE], x_side, x_corner, absent=True)
-        for dst in range(1, nblock):
-            wait_axis(xrsem.at[XSPARE + 1 + dst], n_row, xr_size, absent=True)
-            wait_axis(xrsem.at[XSPARE + 2 + nblock + dst], n_col, xc_size, absent=True)
+                wait_all(rsem.at[(2 + dst) * seqs + s], msg_side, msg_side, msg_corner, absent=True)
         wait_rows(rsem.at[(2 + nblock) * seqs], msg_total)
-        wait_rows(xrsem.at[XSPARE + 1 + nblock], 2 * xr_size)
-        wait_rows(xrsem.at[XSPARE + 2 + 2 * nblock], 2 * xc_size)
         for s in range(seqs):
             cout[s] = cms[s][pl.ds(ring * cols, rows * cols), :]
 
@@ -474,7 +465,7 @@
         + [pltpu.VMEM(((rows + 2 * ring) * cols, hid), F32)] * 2
         + [pltpu.VMEM((nstrip * 32, hid), F32)] * 2
         + [
-            pltpu.VMEM(((2 * nblock + 1) * BLOCK * seqs, pitch, (rows + 16) * chan), F32),
+            pltpu.VMEM((steps * seqs, pitch, (rows + 16) * chan), F32),
             pltpu.VMEM((steps * seqs, rows * chan, cols), BF16),
             pltpu.VMEM((kdim, gates), BF16),
         ]
@@ -490,12 +481,16 @@
             pltpu.VMEM((3 + nblock, seqs, 4, 80, hid), BF16),
             pltpu.VMEM((3 + nblock, seqs, 4, ring * cols, hid), F32),
             pltpu.VMEM((3 + nblock, seqs, 4, 16, hid), F32),
+            pltpu.VMEM((nblock, 2, 16, rows * chan), BF16),
+            pltpu.VMEM((nblock, 2, 16, (rows + 16) * chan), BF16),
+            pltpu.VMEM((2, 16, rows * chan), F32),
+            pltpu.VMEM((2, 16, (rows + 16) * chan), F32),
             pltpu.VMEM((2, 32, hid), F32),
             pltpu.SemaphoreType.DMA((8,)),
             pltpu.SemaphoreType.DMA((seqs,)),
             pltpu.SemaphoreType.DMA(((3 + nblock) * seqs,)),
-            pltpu.SemaphoreType.DMA((3,)),
-            pltpu.SemaphoreType.DMA((8 + 2 * nblock,)),
+            pltpu.SemaphoreType.DMA((2,)),
+            pltpu.SemaphoreType.DMA((2,)),
         ]
     )
     return kernel, scratch

time: 59.2 us -> 49 us (0.83)
  Pallas kernels: 55.9 us -> 45.7 us
    pallas_call x1, Pallas kernels: 55.9 us -> 45.7 us  [local_run(): pl.pallas_call(kernel, out_shape=(pltpu.VMEM((steps, seqs, rows * cols, h...]
where the time goes in v4:
time: 49 us; the launch traced here: 48.9 us
  Pallas kernels  45.7 us (93%)
  local copies, waits for them, and re-layouts  2.61 us (5%)
  between operations  0.64 us (1%)
    pallas_call x1, Pallas kernels, local_run(): pl.pallas_call(kernel, out_shape=(pltpu.VMEM((steps, seqs, rows * cols, h...  45.7 us
    unnamed x2, local copies, waits for them, and re-layouts  2.61 us

profile of v4, /device:TPU:97, one launch (start us, length us, event | category | flops | bytes accessed | tf_op | source)
XLA Modules:
  0.0 48.9 jit_solution(10278282272858250322)
XLA Ops:
  0.6 45.7 %shard_map.77 = (bf16[12,2,576,128]{3,2,1,0:T(8,128)(2,1)S(1)}, f32[2,576,128]{2,1,0:T(8,128)S(1)}) custom-call(bf16[24,384,24]{2,1,0:T(8,128)(2,1)} %bitcast.11, bf16[3,3,16,512]{3,2,1,0:T(8,128)(2,1)} %wx_hbm.1, bf16[1152,512]{1,0:T(8,128)(2,1)} %bitcast.12, f32[1,512]{1,0:T(1,128)} %bitcast.15, bf16[2,576,128]{2,1,0:T(8,128)(2,1)} %bitcast.14, ...), custom_call_target="tpu_custom_call" | custom-call | tf_op jit(solution)/shard_map/pallas_call | solution.py:513
  46.3 1.8 %copy.10 = bf16[12,2,24,24,128]{4,3,2,1,0:T(8,128)(2,1)} copy(bf16[12,2,24,24,128]{4,3,2,1,0:T(8,128)(2,1)S(1)} %bitcast.9) | data formatting | bytes 7077888
  48.1 0.8 %copy.11 = f32[2,24,24,128]{3,2,1,0:T(8,128)} copy(f32[2,24,24,128]{3,2,1,0:T(8,128)S(1)} %bitcast.10) | data formatting | bytes 1179648

commit v5 on v4

--- a/solution.py
+++ b/solution.py
@@ -67,9 +67,8 @@
                 out = jnp.logical_and(out, extra)
             return out
 
-        def dev(k, dst=0):
-            real = jnp.logical_and(present[k], dst < nblock)
-            return {"rows": jnp.where(real, ri + DIRS[k][0], partner), "cols": jnp.where(real, ci + DIRS[k][1], ci)}
+        def dev(k):
+            return {"rows": jnp.where(present[k], ri + DIRS[k][0], partner), "cols": jnp.where(present[k], ci + DIRS[k][1], ci)}
 
         present = [exists(k) for k in range(8)]
         partner = jnp.where(lax.rem(ri, 2) == 0, ri + 1, ri - 1)
@@ -78,8 +77,8 @@
 
         p_row = jnp.where(partner > 0, 1, 0) + jnp.where(partner < row_count - 1, 1, 0)
 
-        def pick(k, dst, real, spare):
-            return jnp.where(jnp.logical_and(present[k], dst < nblock), real, spare)
+        def pick(k, real, spare):
+            return jnp.where(present[k], real, spare)
 
         def h_addr(r, c):
             return (r + BLOCK) * pitch + COL0 + c
@@ -105,20 +104,9 @@
         cp_g.start()
 
         barrier = pltpu.get_barrier_semaphore()
-        for ref in (rh, rc, rq):
-            ref[pl.ds(0, 2)] = jnp.zeros((2,) + ref.shape[1:], ref.dtype)
-        xr[...] = jnp.zeros_like(xr)
-
-        xlanes = xt.shape[2]
-
-        def zero_x(i, _):
-            for lane0 in (0, xlanes - 128):
-                xt[i, pl.ds(COL0, cols), pl.ds(lane0, 128)] = jnp.zeros((cols, 128), F32)
-            return 0
-
-        lax.fori_loop(0, steps * seqs, zero_x, 0)
         for k in range(8):
             pl.semaphore_signal(barrier, 1, device_id=dev(k), device_id_type=MESH)
+
         top_ok = jnp.where(ri > 0, 1.0, 0.0).astype(F32)
         bot_ok = jnp.where(ri < row_count - 1, 1.0, 0.0).astype(F32)
         left_ok = jnp.where(ci > 0, 1.0, 0.0).astype(F32)
@@ -132,14 +120,14 @@
         pl.semaphore_wait(barrier, met + 8 - ((p_row + 1) * (n_col + 1) - 1))
 
         def msg_copies(s, k, dst):
-            slot = pick(k, dst, lax.rem(dst, 2), 2 + dst)
-            sem = pick(k, dst, lax.rem(dst, 2) * seqs + s, 2 * seqs + dst * seqs + s)
+            slot = pick(k, lax.rem(dst, 2), 2 + dst)
+            sem = pick(k, lax.rem(dst, 2) * seqs + s, 2 * seqs + dst * seqs + s)
             if k < 4:
                 pairs = ((sh.at[s, k], rh.at[slot, s, k]), (sc.at[s, k], rc.at[slot, s, k]))
             else:
                 pairs = ((sq.at[s, k - 4], rq.at[slot, s, k - 4]),)
             return [
-                pltpu.make_async_remote_copy(src_ref=a, dst_ref=b, send_sem=ssem.at[s], recv_sem=rsem.at[sem], device_id=dev(k, dst), device_id_type=MESH)
+                pltpu.make_async_remote_copy(src_ref=a, dst_ref=b, send_sem=ssem.at[s], recv_sem=rsem.at[sem], device_id=dev(k), device_id_type=MESH)
                 for a, b in pairs
             ]
 
@@ -196,9 +184,11 @@
                         cs[pl.ds((st0 + j) * 32 + q0, ring), :] = rq[par, s, o - 4, pl.ds(BLOCK * BLOCK + j * ring, ring), :]
 
         def send(s, dst):
-            for k in range(8):
-                for cp in msg_copies(s, k, dst):
-                    cp.start()
+            for k in (4, 5, 6, 7):
+                msg_copies(s, k, dst)[0].start()
+            for n in range(2):
+                for k in (2, 3, 0, 1):
+                    msg_copies(s, k, dst)[n].start()
 
         def wait_rows(sem, n):
             pltpu.make_async_copy(cinit.at[:, pl.ds(0, n // seqs)], cout.at[:, pl.ds(0, n // seqs)], sem).wait()
@@ -298,6 +288,8 @@
         send_x(0, 1, 0)
         load_state(1)
         cp_c[1].wait()
+        pack(1)
+        send(1, 0)
         cp_w.wait()
         for cp in cp_small:
             cp.wait()
@@ -315,6 +307,32 @@
 
         lax.fori_loop(1, nblock, prep_more, 0)
         send_x(1, nblock - 1, 1)
+        for k in range(8):
+            o = opposite(k)
+
+            @pl.when(jnp.logical_not(present[k]))
+            def _():
+                for par in range(2):
+                    for s in range(seqs):
+                        if k < 4:
+                            rh[par, s, o] = jnp.zeros(rh.shape[3:], BF16)
+                            rc[par, s, o] = jnp.zeros(rc.shape[3:], F32)
+                        else:
+                            rq[par, s, o - 4] = jnp.zeros(rq.shape[3:], F32)
+                dr, dc = DIRS[k]
+                if dc == 0:
+                    lane0 = 0 if dr < 0 else own_lane + row_lanes
+
+                    def zero_x(i, _):
+                        xt[i, pl.ds(COL0, cols), pl.ds(lane0, 128)] = jnp.zeros((cols, 128), F32)
+                        return 0
+
+                    lax.fori_loop(0, steps * seqs, zero_x, 0)
+                else:
+                    lane0 = {-1: 0, 0: own_lane, 1: own_lane + row_lanes}[dr]
+                    n = row_lanes if dr == 0 else 128
+                    xr[:, 0 if dc < 0 else 1, :, pl.ds(lane0, n)] = jnp.zeros((nblock, 16, n), BF16)
+
         wait_all(xrsem.at[0], *x_sizes)
         unpack_x(0)
         lane = lax.broadcasted_iota(jnp.int32, (pitch, 128), 1)
@@ -332,13 +350,13 @@
                         v = jnp.where(lane < 128 - chan * off, v, w)
                 xg[pl.ds(x_addr(r, -COL0), pitch), :] = v
 
-        def build_lhs(s, j, ch):
+        def build_lhs(s, j, ch, taps=tuple(range(12))):
             hb = hbs[s][j]
             xg = xgs[s]
             r0, nr, strips = chunk_list(BLOCK - 1 - j)[ch]
             lhs = lhss[ch]
             base = 32 * len(strips)
-            for tap in range(12):
+            for tap in taps:
                 for n, k in enumerate(strips):
                     if tap < 9:
                         dr, dc = tap // 3 - 1, tap % 3 - 1
@@ -346,16 +364,33 @@
                     else:
                         v = xg[pl.ds(x_addr(-ring, strip_cols[k] + tap - 10), 32, stride=pitch), :]
                     lhs[pl.ds(32 * n, 32), pl.ds(tap * 128, 128)] = v.astype(BF16)
-                for i in range(0, nr, 2):
-                    pieces = []
-                    for r in range(r0 + i, min(r0 + i + 2, r0 + nr)):
-                        if tap < 9:
-                            dr, dc = tap // 3 - 1, tap % 3 - 1
-                            pieces.append(hb[pl.ds(h_addr(r + dr, dc), cols), :])
+
+            def rows_of(ref, addr, r, cnt, dc):
+                v = [ref[pl.ds(addr(r + i, dc), cols), :] for i in range(cnt)]
+                return (jnp.concatenate(v, axis=0) if cnt > 1 else v[0]).astype(BF16)
+
+            def put(tap, i, cnt, v):
+                lhs[pl.ds(base + i * cols, cnt * cols), pl.ds(tap * 128, 128)] = v
+
+            pairs = [(i, min(2, nr - i)) for i in range(0, nr, 2)]
+            for dc in (-1, 0, 1):
+                if dc + 10 in taps:
+                    for i, cnt in pairs:
+                        put(dc + 10, i, cnt, rows_of(xg, x_addr, r0 + i, cnt, dc))
+                if dc + 1 in taps:
+                    for i, cnt in pairs:
+                        put(dc + 4, i, cnt, rows_of(hb, h_addr, r0 + i, cnt, dc))
+                        if cnt == 2:
+                            v = rows_of(hb, h_addr, r0 + i - 1, 2, dc)
+                            put(dc + 1, i, 2, v)
+                            if i:
+                                put(dc + 7, i - 2, 2, v)
                         else:
-                            pieces.append(xg[pl.ds(x_addr(r, tap - 10), cols), :])
-                    v = jnp.concatenate(pieces, axis=0) if len(pieces) > 1 else pieces[0]
-                    lhs[pl.ds(base + i * cols, len(pieces) * cols), pl.ds(tap * 128, 128)] = v.astype(BF16)
+                            v = rows_of(hb, h_addr, r0 + i - 1, 2, dc)
+                            put(dc + 7, i - 2, 2, v)
+                            put(dc + 1, i, 1, rows_of(hb, h_addr, r0 + i - 1, 1, dc))
+                    i, cnt = pairs[-1]
+                    put(dc + 7, i, cnt, rows_of(hb, h_addr, r0 + i + 1, cnt, dc))
 
         def matmul(j, ch):
             r0, nr, strips = chunk_list(BLOCK - 1 - j)[ch]
@@ -371,7 +406,7 @@
             c_new = acts[1] * c + acts[0] * acts[3]
             return acts[2] * jnp.tanh(c_new), c_new
 
-        def elementwise(s, j, ch, t, skip=None):
+        def elementwise(s, j, ch, t):
             ext = BLOCK - 1 - j
             dst = hbs[s][(j + 1) % BLOCK]
             r0, nr, strips = chunk_list(ext)[ch]
@@ -388,8 +423,6 @@
                 crow = (r + ring) * cols
                 c_old = cms[s][pl.ds(crow, cnt * cols), :]
                 h, c_new = cell(gss[ch], base + (r - r0) * cols, cnt * cols, c_old)
-                if skip is not None:
-                    c_new = jnp.where(skip, c_old, c_new)
                 cms[s][pl.ds(crow, cnt * cols), :] = c_new
                 if not inside:
                     h = h * (top_ok if r < 0 else bot_ok)
@@ -398,37 +431,19 @@
                     hout[t, s, pl.ds(r * cols, cnt * cols), :] = hb16
                 h = hb16.astype(F32)
                 for i in range(cnt):
-                    new = h[i * cols:(i + 1) * cols]
-                    if skip is not None:
-                        new = jnp.where(skip, dst[pl.ds(h_addr(r + i, 0), cols), :], new)
-                    dst[pl.ds(h_addr(r + i, 0), cols), :] = new
+                    dst[pl.ds(h_addr(r + i, 0), cols), :] = h[i * cols:(i + 1) * cols]
                 r += cnt
-
-        last = (BLOCK - 1, 2)
 
         def block(b, _):
             par = lax.rem(b, 2)
             for s in range(seqs):
                 o = 1 - s
                 wait_all(rsem.at[par * seqs + s], msg_side, msg_side, msg_corner)
-                if s == 0:
-                    @pl.when(b > 0)
-                    def _():
-                        wait_rows(ssem.at[o], msg_total)
-                else:
-                    wait_rows(ssem.at[o], msg_total)
+                wait_rows(ssem.at[s], msg_total)
+                if s > 0:
                     wait_all(xrsem.at[1], *[(nblock - 1) * n for n in x_sizes], more=b == 0)
                 unpack(s, par)
-                build_xg(s, b * BLOCK, BLOCK - 1)
-                build_lhs(s, 0, 0)
-                if s == 0:
-                    elementwise(o, *last, lax.rem(b * BLOCK - 1 + steps, steps), b == 0)
-                    pack(o)
-                    send(o, b)
-                else:
-                    elementwise(o, *last, b * BLOCK + BLOCK - 1)
-                    pack(o)
-                    send(o, b + 1)
+                build_lhs(s, 0, 0, tuple(range(9)))
                 late = None
                 for j in range(BLOCK):
                     if j > 0:
@@ -442,18 +457,25 @@
                         if late is not None:
                             elementwise(s, *late, b * BLOCK + late[0])
                         late = (j, ch)
+                    if j == BLOCK - 1:
+                        build_xg(o, lax.rem((b + s) * BLOCK, steps), BLOCK - 1)
+                        build_lhs(o, 0, 0, (9, 10, 11))
+                elementwise(s, *late, b * BLOCK + late[0])
+
+                @pl.when(b < nblock - 1)
+                def _():
+                    pack(s)
+                    send(s, b + 1)
             return 0
 
+        build_xg(0, 0, BLOCK - 1)
+        build_lhs(0, 0, 0, (9, 10, 11))
         lax.fori_loop(0, nblock, block, 0)
-        elementwise(1, *last, steps - 1)
-        wait_rows(ssem.at[0], msg_total)
-        wait_rows(ssem.at[1], msg_total)
         wait_all(xssem.at[0], *x_sizes)
         wait_all(xssem.at[1], *[(nblock - 1) * n for n in x_sizes])
         for dst in range(nblock):
             for s in range(seqs):
                 wait_all(rsem.at[(2 + dst) * seqs + s], msg_side, msg_side, msg_corner, absent=True)
-        wait_rows(rsem.at[(2 + nblock) * seqs], msg_total)
         for s in range(seqs):
             cout[s] = cms[s][pl.ds(ring * cols, rows * cols), :]
 
@@ -478,9 +500,9 @@
             pltpu.VMEM((seqs, 4, 80, hid), BF16),
             pltpu.VMEM((seqs, 4, ring * cols, hid), F32),
             pltpu.VMEM((seqs, 4, 16, hid), F32),
-            pltpu.VMEM((3 + nblock, seqs, 4, 80, hid), BF16),
-            pltpu.VMEM((3 + nblock, seqs, 4, ring * cols, hid), F32),
-            pltpu.VMEM((3 + nblock, seqs, 4, 16, hid), F32),
+            pltpu.VMEM((2 + nblock, seqs, 4, 80, hid), BF16),
+            pltpu.VMEM((2 + nblock, seqs, 4, ring * cols, hid), F32),
+            pltpu.VMEM((2 + nblock, seqs, 4, 16, hid), F32),
             pltpu.VMEM((nblock, 2, 16, rows * chan), BF16),
             pltpu.VMEM((nblock, 2, 16, (rows + 16) * chan), BF16),
             pltpu.VMEM((2, 16, rows * chan), F32),
@@ -488,7 +510,7 @@
             pltpu.VMEM((2, 32, hid), F32),
             pltpu.SemaphoreType.DMA((8,)),
             pltpu.SemaphoreType.DMA((seqs,)),
-            pltpu.SemaphoreType.DMA(((3 + nblock) * seqs,)),
+            pltpu.SemaphoreType.DMA(((2 + nblock) * seqs,)),
             pltpu.SemaphoreType.DMA((2,)),
             pltpu.SemaphoreType.DMA((2,)),
         ]

time: 49 us -> 46.3 us (0.945)
  Pallas kernels: 45.7 us -> 43 us
    pallas_call x1, Pallas kernels: 45.7 us -> 43 us  [local_run(): pl.pallas_call(kernel, out_shape=(pltpu.VMEM((steps, seqs, rows * cols, h...]
where the time goes in v5:
time: 46.3 us
  Pallas kernels  43 us (93%)
  local copies, waits for them, and re-layouts  2.61 us (6%)
  between operations  0.64 us (1%)
    pallas_call x1, Pallas kernels, local_run(): pl.pallas_call(kernel, out_shape=(pltpu.VMEM((steps, seqs, rows * cols, h...  43 us
    unnamed x2, local copies, waits for them, and re-layouts  2.61 us

profile of v5, /device:TPU:97, one launch (start us, length us, event | category | flops | bytes accessed | tf_op | source)
XLA Modules:
  0.0 46.3 jit_solution(4351741857153778856)
XLA Ops:
  0.6 43.0 %shard_map.77 = (bf16[12,2,576,128]{3,2,1,0:T(8,128)(2,1)S(1)}, f32[2,576,128]{2,1,0:T(8,128)S(1)}) custom-call(bf16[24,384,24]{2,1,0:T(8,128)(2,1)} %bitcast.11, bf16[3,3,16,512]{3,2,1,0:T(8,128)(2,1)} %wx_hbm.1, bf16[1152,512]{1,0:T(8,128)(2,1)} %bitcast.12, f32[1,512]{1,0:T(1,128)} %bitcast.15, bf16[2,576,128]{2,1,0:T(8,128)(2,1)} %bitcast.14, ...), custom_call_target="tpu_custom_call" | custom-call | tf_op jit(solution)/shard_map/pallas_call | solution.py:535
  43.6 1.8 %copy.10 = bf16[12,2,24,24,128]{4,3,2,1,0:T(8,128)(2,1)} copy(bf16[12,2,24,24,128]{4,3,2,1,0:T(8,128)(2,1)S(1)} %bitcast.9) | data formatting | bytes 7077888
  45.4 0.8 %copy.11 = f32[2,24,24,128]{3,2,1,0:T(8,128)} copy(f32[2,24,24,128]{3,2,1,0:T(8,128)S(1)} %bitcast.10) | data formatting | bytes 1179648

commit v6 on v5

--- a/solution.py
+++ b/solution.py
@@ -115,9 +115,6 @@
         rmask = jnp.where(srow < ring, top_ok, jnp.where(srow >= rows + ring, bot_ok, 1.0))
         smask[0] = rmask * left_ok
         smask[1] = rmask * right_ok
-
-        met = (n_row + 1) * (n_col + 1) - 1
-        pl.semaphore_wait(barrier, met + 8 - ((p_row + 1) * (n_col + 1) - 1))
 
         def msg_copies(s, k, dst):
             slot = pick(k, lax.rem(dst, 2), 2 + dst)
@@ -263,7 +260,6 @@
         load_state(0)
         cp_c[0].wait()
         pack(0)
-        send(0, 0)
 
         eye = (lax.broadcasted_iota(jnp.int32, (cols, cols), 0) == lax.broadcasted_iota(jnp.int32, (cols, cols), 1)).astype(F32).astype(BF16)
 
@@ -278,6 +274,10 @@
         cp_f.wait()
         prep_x(0)
         pack_x(0)
+        met = (n_row + 1) * (n_col + 1) - 1
+        pl.semaphore_wait(barrier, met + 8 - ((p_row + 1) * (n_col + 1) - 1))
+
+        send(0, 0)
 
         def send_x(first, count, sem):
             for k in range(8):

time: 46.3 us -> 46.3 us (level)
  no operation moved by 1% of the time
where the time goes in v6:
time: 46.3 us; the launch traced here: 46.2 us
  Pallas kernels  42.9 us (93%)
  local copies, waits for them, and re-layouts  2.61 us (6%)
  between operations  0.64 us (1%)
    pallas_call x1, Pallas kernels, local_run(): pl.pallas_call(kernel, out_shape=(pltpu.VMEM((steps, seqs, rows * cols, h...  42.9 us
    unnamed x2, local copies, waits for them, and re-layouts  2.61 us

profile of v6, /device:TPU:97, one launch (start us, length us, event | category | flops | bytes accessed | tf_op | source)
XLA Modules:
  0.0 46.2 jit_solution(15500184045259882136)
XLA Ops:
  0.6 42.9 %shard_map.77 = (bf16[12,2,576,128]{3,2,1,0:T(8,128)(2,1)S(1)}, f32[2,576,128]{2,1,0:T(8,128)S(1)}) custom-call(bf16[24,384,24]{2,1,0:T(8,128)(2,1)} %bitcast.11, bf16[3,3,16,512]{3,2,1,0:T(8,128)(2,1)} %wx_hbm.1, bf16[1152,512]{1,0:T(8,128)(2,1)} %bitcast.12, f32[1,512]{1,0:T(1,128)} %bitcast.15, bf16[2,576,128]{2,1,0:T(8,128)(2,1)} %bitcast.14, ...), custom_call_target="tpu_custom_call" | custom-call | tf_op jit(solution)/shard_map/pallas_call | solution.py:535
  43.6 1.8 %copy.10 = bf16[12,2,24,24,128]{4,3,2,1,0:T(8,128)(2,1)} copy(bf16[12,2,24,24,128]{4,3,2,1,0:T(8,128)(2,1)S(1)} %bitcast.9) | data formatting | bytes 7077888
  45.4 0.8 %copy.11 = f32[2,24,24,128]{3,2,1,0:T(8,128)} copy(f32[2,24,24,128]{3,2,1,0:T(8,128)S(1)} %bitcast.10) | data formatting | bytes 1179648
